TPU v7x, 32 devices: a 4x4x1 block of a 4x4x8 slice. The times are simulated.
32 devices in a mesh: rep: 1 (over z), y: 4 (over y), x: 8 (over x, core).
Axes of the slice: x: 4, y: 4, z: 1, core: 2. Of those that a mesh axis runs over, the one named last changes fastest.
The devices are a block of a 4x4x8 slice.
Arguments:
- hidden: bfloat16 [64, 4096], P('rep', 'y')
- lengths: int32 [64], P('rep')
- k_cache: bfloat16 [2, 64, 128, 32, 128], P(None, ('rep', 'y'), None, 'x')
- v_cache: bfloat16 [2, 64, 128, 32, 128], P(None, ('rep', 'y'), None, 'x')
- rel_table: bfloat16 [2, 128, 32, 128], P(None, None, 'x')
- norm_attn: bfloat16 [2, 4096], P(None, 'y')
- w_q: bfloat16 [2, 4096, 32, 128], P(None, 'y', 'x')
- w_k: bfloat16 [2, 4096, 32, 128], P(None, 'y', 'x')
- w_v: bfloat16 [2, 4096, 32, 128], P(None, 'y', 'x')
- bias_content: bfloat16 [2, 32, 128], P(None, 'x')
- bias_pos: bfloat16 [2, 32, 128], P(None, 'x')
- w_out: bfloat16 [2, 32, 128, 4096], P(None, 'x', None, 'y')
- norm_mlp: bfloat16 [2, 4096], P(None, 'y')
- w_up: bfloat16 [2, 4096, 16384], P(None, 'y', 'x')
- w_down: bfloat16 [2, 16384, 4096], P(None, 'x', 'y')
Outputs:
- output 1: bfloat16 [64, 4096], P('rep', 'y')
- output 2: bfloat16 [2, 64, 128, 32, 128], P(None, ('rep', 'y'), None, 'x')
- output 3: bfloat16 [2, 64, 128, 32, 128], P(None, ('rep', 'y'), None, 'x')
All inputs are finite; a program needn't handle non-finite values.
Results may differ from a plain program's by a relative error of at most 0.02.
Values are sent between devices in bfloat16 or wider.
A program may use at most 768 MiB of HBM per device.

v0:
```python
import jax
import jax.numpy as jnp
from jax import lax
from jax.sharding import PartitionSpec as P

EPS = 1e-6


def sharded_norm(hidden, gain, d_total):
    hidden_wide = hidden.astype(jnp.float32)
    sum_sq = lax.psum(jnp.sum(hidden_wide * hidden_wide, axis=1, keepdims=True), "y")
    inv_rms = lax.rsqrt(sum_sq / d_total + EPS)
    return (hidden_wide * inv_rms * gain.astype(jnp.float32)).astype(jnp.bfloat16)


def shift_rel(rel_all, lengths):
    seq_len = rel_all.shape[2]
    padded = jnp.pad(rel_all[:, :, ::-1], ((0, 0), (0, 0), (0, seq_len)))
    return jax.vmap(lambda rel_row, start_at: lax.dynamic_slice_in_dim(rel_row, start_at, seq_len, axis=1))(padded, seq_len - 1 - lengths)


def write_rows(cache_layer, new_rows, lengths):
    hit_mask = jnp.arange(cache_layer.shape[1])[None, :] == lengths[:, None]
    return jnp.where(hit_mask[:, :, None, None], new_rows[:, None, :, :], cache_layer)


def attend(q_rows, k_rows, v_rows, lengths, rel_layer, content_bias, pos_bias):
    q_wide = q_rows.astype(jnp.float32)
    q_content = (q_wide + content_bias.astype(jnp.float32)).astype(jnp.bfloat16)
    q_pos = (q_wide + pos_bias.astype(jnp.float32)).astype(jnp.bfloat16)
    scores = jnp.einsum("bhe,bshe->bhs", q_content, k_rows, preferred_element_type=jnp.float32)
    rel_all = jnp.einsum("bhe,the->bht", q_pos, rel_layer, preferred_element_type=jnp.float32)
    scores = (scores + shift_rel(rel_all, lengths)) * (q_rows.shape[2] ** -0.5)
    in_range = jnp.arange(k_rows.shape[1])[None, None, :] <= lengths[:, None, None]
    attn_prob = jax.nn.softmax(jnp.where(in_range, scores, -1e30), axis=-1).astype(jnp.bfloat16)
    return jnp.einsum("bhs,bshe->bhe", attn_prob, v_rows, preferred_element_type=jnp.float32).astype(jnp.bfloat16)


def solution(mesh):
    y_size = mesh.shape["y"]
    cache_spec = P(None, ("rep", "y"), None, "x", None)
    row_spec = P("rep", "y")
    proj_spec = P(None, "y", "x", None)
    head_spec = P(None, "x", None)
    in_specs = (row_spec, P("rep"), cache_spec, cache_spec, P(None, None, "x", None), P(None, "y"),
                proj_spec, proj_spec, proj_spec, head_spec, head_spec, P(None, "x", None, "y"),
                P(None, "y"), P(None, "y", "x"), P(None, "x", "y"))
    out_specs = (row_spec, cache_spec, cache_spec)

    def local_step(hidden, lengths, k_cache, v_cache, rel_table, norm_attn, w_q, w_k, w_v, bias_content, bias_pos, w_out, norm_mlp, w_up, w_down):
        rows_local = k_cache.shape[1]
        row_start = lax.axis_index("y") * rows_local
        len_local = lax.dynamic_slice_in_dim(lengths, row_start, rows_local)
        d_total = hidden.shape[1] * y_size
        k_layers = []
        v_layers = []
        for layer in range(k_cache.shape[0]):
            normed = sharded_norm(hidden, norm_attn[layer], d_total)
            q_part = jnp.einsum("bd,dhe->bhe", normed, w_q[layer], preferred_element_type=jnp.float32).astype(jnp.bfloat16)
            k_part = jnp.einsum("bd,dhe->bhe", normed, w_k[layer], preferred_element_type=jnp.float32).astype(jnp.bfloat16)
            v_part = jnp.einsum("bd,dhe->bhe", normed, w_v[layer], preferred_element_type=jnp.float32).astype(jnp.bfloat16)
            q_full, k_full, v_full = lax.psum((q_part, k_part, v_part), "y")
            q_rows = lax.dynamic_slice_in_dim(q_full, row_start, rows_local)
            k_rows = lax.dynamic_slice_in_dim(k_full, row_start, rows_local)
            v_rows = lax.dynamic_slice_in_dim(v_full, row_start, rows_local)
            k_new = write_rows(k_cache[layer], k_rows, len_local)
            v_new = write_rows(v_cache[layer], v_rows, len_local)
            k_layers.append(k_new)
            v_layers.append(v_new)
            context = attend(q_rows, k_new, v_new, len_local, rel_table[layer], bias_content[layer], bias_pos[layer])
            context_all = lax.all_gather(context, "y", axis=0, tiled=True)
            attn_part = jnp.einsum("bhe,hed->bd", context_all, w_out[layer], preferred_element_type=jnp.float32).astype(jnp.bfloat16)
            attn_out = lax.psum(attn_part, "x")
            hidden = (hidden.astype(jnp.float32) + attn_out.astype(jnp.float32)).astype(jnp.bfloat16)
            normed = sharded_norm(hidden, norm_mlp[layer], d_total)
            up_part = jnp.dot(normed, w_up[layer], preferred_element_type=jnp.float32).astype(jnp.bfloat16)
            up_proj = lax.psum(up_part, "y")
            activated = jax.nn.gelu(up_proj.astype(jnp.float32), approximate=True).astype(jnp.bfloat16)
            down_part = jnp.dot(activated, w_down[layer], preferred_element_type=jnp.float32).astype(jnp.bfloat16)
            down_out = lax.psum(down_part, "x")
            hidden = (hidden.astype(jnp.float32) + down_out.astype(jnp.float32)).astype(jnp.bfloat16)
        return hidden, jnp.stack(k_layers), jnp.stack(v_layers)

    return jax.shard_map(local_step, mesh=mesh, in_specs=in_specs, out_specs=out_specs, check_vma=False)
```

profile of v0, /device:TPU:97, one launch (start us, length us, event | category | flops | bytes accessed | tf_op | source)
XLA Modules:
  0.0 520.2 jit_solution(925508503846745890)
XLA Ops:
  7.2 1.0 fusion.58
  8.3 11.2 %psum.112 = f32[64,1]{0,1:T(1,128)S(1)} all-reduce(f32[64,1]{0,1:T(1,128)S(1)} %bitcast.155), channel_id=1, replica_groups=mesh['rep'=1,'y'=4,'x'=8] {'y'}, use_global_device_ids=true, to_apply=%region_1.0 | all-reduce | flops 64 | bytes 512 | tf_op jit(solution)/shard_map/psum | solution.py:11
  19.5 1.4 slice_convert_fusion.1
  20.9 3.4 fusion.129
  24.3 1.7 fusion.128
  26.0 1.0 convolution_convert_fusion.5
  26.9 1.0 convolution_convert_fusion.4
  27.9 1.7 fusion.127
  29.6 1.0 convolution_convert_fusion.3
  31.0 0.7 fusion.130
  31.8 34.9 %all-reduce.28.cloned.1.call-done = (bf16[64,4,128]{2,0,1:T(8,128)(2,1)}, bf16[64,4,128]{2,0,1:T(8,128)(2,1)}, bf16[64,4,128]{2,0,1:T(8,128)(2,1)}) async-done(((bf16[64,4,128]{2,0,1:T(8,128)(2,1)}, bf16[64,4,128]{2,0,1:T(8,128)(2,1)}, bf16[64,4,128]{2,0,1:T(8,128)(2,1)}), (bf16[64,4,128]{2,0,1:T(8,128)(2,1)}, bf16[64,4,128]{2,0,1:T(8,128)(2,1)}, ...) | async-done | bytes 196624 | tf_op jit(solution)/shard_map/psum | solution.py:62
  66.7 0.9 convolution_bitcast_fusion.3
  67.7 0.8 constant_dynamic-slice_fusion.1
  68.5 0.7 fusion.97
  69.2 0.5 copy.87
  69.9 2.1 gather_fusion
  72.0 7.1 %multiply_reduce_fusion.1 = f32[16,4,128]{1,2,0:T(8,128)S(1)} fusion(f32[16,4,128]{2,1,0:T(4,128)S(1)} %copy.85, pred[16,128]{1,0:T(8,128)(4,1)S(1)} %get-tuple-element.40, bf16[2,16,128,4,128]{4,3,2,1,0:T(4,128)(2,1)} %param.17, bf16[16,4,128]{2,1,0:T(4,128)(2,1)S(1)} %copy.41), kind=kLoop, calls=%fused_computation.13 | loop fusion | flops 4186112 | bytes 2181120
  79.2 1.3 fusion.125
  80.5 0.2 fusion.40
  80.9 0.5 copy.64
  81.4 5.6 %bitcast_select_fusion.2 = bf16[16,128,4,128]{3,2,1,0:T(4,128)(2,1)S(1)} fusion(pred[16,128]{1,0:T(8,128)(4,1)S(1)} %get-tuple-element.40, bf16[2,16,128,4,128]{4,3,2,1,0:T(4,128)(2,1)} %param.18, bf16[16,4,128]{2,1,0:T(4,128)(2,1)S(1)} %copy.45), kind=kLoop, calls=%fused_computation.23 | loop fusion | flops 1048576 | bytes 4212736 | tf_op jit(solution)/shard_map/jit(_where)/select_n | solution.py:24
  87.1 0.6 fusion.22
  87.7 9.0 %all_gather.6 = bf16[64,4,128]{2,0,1:T(8,128)(2,1)S(1)} all-gather(bf16[16,4,128]{2,0,1:T(8,128)(2,1)S(1)} %bitcast.144), channel_id=1, replica_groups=mesh['rep'=1,'y'=4,'x'=8] {'y'}, dimensions={0}, use_global_device_ids=true | all-gather | bytes 81920 | tf_op jit(solution)/shard_map/all_gather | solution.py:71
  96.7 1.0 fusion.24
  97.8 0.6 slice_convert_fusion.2
  98.4 56.7 %all-reduce.14.cloned.1.call-done = bf16[64,1024]{1,0:T(8,128)(2,1)} async-done(((bf16[64,1024]{1,0:T(8,128)(2,1)}), bf16[64,1024]{1,0:T(8,128)(2,1)}) %all-reduce.14.cloned.1.call-update) | async-done | bytes 131088 | tf_op jit(solution)/shard_map/psum | solution.py:73
  155.2 1.0 fusion.62
  156.2 8.5 %psum.117 = f32[64,1]{0,1:T(1,128)S(1)} all-reduce(f32[64,1]{0,1:T(1,128)S(1)} %bitcast.156), channel_id=1, replica_groups=mesh['rep'=1,'y'=4,'x'=8] {'y'}, use_global_device_ids=true, to_apply=%region_9.10 | all-reduce | flops 64 | bytes 512 | tf_op jit(solution)/shard_map/psum | solution.py:11
  164.8 3.9 fusion.12
  168.8 35.6 %all-reduce.16.cloned.1.call-done = bf16[64,2048]{1,0:T(8,128)(2,1)} async-done(((bf16[64,2048]{1,0:T(8,128)(2,1)}), bf16[64,2048]{1,0:T(8,128)(2,1)}) %all-reduce.16.cloned.1.call-update) | async-done | bytes 262160 | tf_op jit(solution)/shard_map/psum | solution.py:77
  204.5 3.8 fusion.26
  208.3 0.2 all-reduce.26.cloned.1.call-start
  208.6 54.9 %all-reduce.18.cloned.1.call-done = bf16[64,1024]{1,0:T(8,128)(2,1)} async-done(((bf16[64,1024]{1,0:T(8,128)(2,1)}), bf16[64,1024]{1,0:T(8,128)(2,1)}) %all-reduce.18.cloned.1.call-update) | async-done | bytes 131088 | tf_op jit(solution)/shard_map/psum | solution.py:80
  263.5 1.6 fusion.66
  265.1 8.6 %psum.120 = f32[64,1]{0,1:T(1,128)S(1)} all-reduce(f32[64,1]{0,1:T(1,128)} %bitcast.154), channel_id=1, replica_groups=mesh['rep'=1,'y'=4,'x'=8] {'y'}, use_global_device_ids=true, to_apply=%region_13.14 | all-reduce | flops 64 | bytes 512 | tf_op jit(solution)/shard_map/psum | solution.py:11
  273.7 1.7 convolution_convert_fusion.1
  275.4 1.6 convolution_convert_fusion
  277.0 1.6 convolution_convert_fusion.2
  278.8 35.6 %all-reduce.26.cloned.1.call-done = (bf16[64,4,128]{2,0,1:T(8,128)(2,1)}, bf16[64,4,128]{2,0,1:T(8,128)(2,1)}, bf16[64,4,128]{2,0,1:T(8,128)(2,1)}) async-done(((bf16[64,4,128]{2,0,1:T(8,128)(2,1)}, bf16[64,4,128]{2,0,1:T(8,128)(2,1)}, bf16[64,4,128]{2,0,1:T(8,128)(2,1)}), (bf16[64,4,128]{2,0,1:T(8,128)(2,1)}, bf16[64,4,128]{2,0,1:T(8,128)(2,1)}, ...) | async-done | bytes 196624 | tf_op jit(solution)/shard_map/psum | solution.py:62
  314.4 0.9 convolution_bitcast_fusion.2
  315.3 0.8 constant_dynamic-slice_fusion
  316.1 0.7 constant_dynamic-slice_fusion.2
  316.8 0.7 fusion.95
  317.6 0.5 copy.88
  318.3 2.1 gather_fusion.1
  320.4 7.1 %multiply_reduce_fusion = f32[16,4,128]{1,2,0:T(8,128)S(1)} fusion(f32[16,4,128]{2,1,0:T(4,128)S(1)} %copy.86, pred[16,128]{1,0:T(8,128)(4,1)S(1)} %get-tuple-element.40, bf16[2,16,128,4,128]{4,3,2,1,0:T(4,128)(2,1)} %param.17, bf16[16,4,128]{2,1,0:T(4,128)(2,1)S(1)} %copy.48), kind=kLoop, calls=%fused_computation.12 | loop fusion | flops 4186112 | bytes 2181120
  327.5 1.3 fusion.122
  329.2 0.5 copy.74
  329.7 5.6 %bitcast_select_fusion = bf16[16,128,4,128]{3,2,1,0:T(4,128)(2,1)S(1)} fusion(pred[16,128]{1,0:T(8,128)(4,1)S(1)} %get-tuple-element.40, bf16[2,16,128,4,128]{4,3,2,1,0:T(4,128)(2,1)} %param.18, bf16[16,4,128]{2,1,0:T(4,128)(2,1)S(1)} %copy.52), kind=kLoop, calls=%fused_computation.20 | loop fusion | flops 1048576 | bytes 4212736 | tf_op jit(solution)/shard_map/jit(_where)/select_n | solution.py:24
  335.4 0.6 fusion.20
  336.1 9.0 %all_gather.7 = bf16[64,4,128]{2,0,1:T(8,128)(2,1)S(1)} all-gather(bf16[16,4,128]{2,0,1:T(8,128)(2,1)S(1)} %bitcast.145), channel_id=1, replica_groups=mesh['rep'=1,'y'=4,'x'=8] {'y'}, dimensions={0}, use_global_device_ids=true | all-gather | bytes 81920 | tf_op jit(solution)/shard_map/all_gather | solution.py:71
  345.1 1.0 fusion.25
  346.2 9.7 %broadcast_select_fusion.1 = (bf16[1,16,128,4,128]{4,3,2,1,0:T(4,128)(2,1)}, bf16[1,16,128,4,128]{4,3,2,1,0:T(4,128)(2,1)}, bf16[1,16,128,4,128]{4,3,2,1,0:T(4,128)(2,1)S(1)}, bf16[1,16,128,4,128]{4,3,2,1,0:T(4,128)(2,1)}) fusion(pred[16,128]{1,0:T(8,128)(4,1)S(1)} %get-tuple-element.40, bf16[2,16,128,4,128]{4,3,2,1,0:T(4,128)(2,1)} %param.18, ...), kind=kLoop, calls=%fused_computation.31 | loop fusion | flops 4194304 | bytes 16844800 | tf_op jit(solution)/shard_map/jit(_where)/select_n | solution.py:24
  355.9 47.6 %all-reduce.20.cloned.1.call-done = bf16[64,1024]{1,0:T(8,128)(2,1)} async-done(((bf16[64,1024]{1,0:T(8,128)(2,1)}), bf16[64,1024]{1,0:T(8,128)(2,1)}) %all-reduce.20.cloned.1.call-update) | async-done | bytes 131088 | tf_op jit(solution)/shard_map/psum | solution.py:73
  403.4 1.0 fusion.70
  404.5 8.5 %psum.125 = f32[64,1]{0,1:T(1,128)S(1)} all-reduce(f32[64,1]{0,1:T(1,128)S(1)} %bitcast.157), channel_id=1, replica_groups=mesh['rep'=1,'y'=4,'x'=8] {'y'}, use_global_device_ids=true, to_apply=%region_21.22 | all-reduce | flops 64 | bytes 512 | tf_op jit(solution)/shard_map/psum | solution.py:11
  413.0 3.9 fusion.15
  417.0 0.3 all-reduce.24.cloned.1.call-start
  417.2 7.4 %pad_maximum_fusion.1 = bf16[2,16,128,4,128]{4,3,2,1,0:T(4,128)(2,1)} fusion(bf16[1,16,128,4,128]{4,3,2,1,0:T(4,128)(2,1)} %get-tuple-element.18, bf16[1,16,128,4,128]{4,3,2,1,0:T(4,128)(2,1)} %get-tuple-element.17), kind=kLoop, calls=%fused_computation.3 | loop fusion | flops 2097152 | bytes 8388608 | tf_op jit(solution)/shard_map/stack | solution.py:82
  424.6 28.1 %all-reduce.22.cloned.1.call-done = bf16[64,2048]{1,0:T(8,128)(2,1)} async-done(((bf16[64,2048]{1,0:T(8,128)(2,1)}), bf16[64,2048]{1,0:T(8,128)(2,1)}) %all-reduce.22.cloned.1.call-update) | async-done | bytes 262160 | tf_op jit(solution)/shard_map/psum | solution.py:77
  452.7 3.8 fusion.29
  456.5 6.8 %pad_maximum_fusion = bf16[2,16,128,4,128]{4,3,2,1,0:T(4,128)(2,1)} fusion(bf16[1,16,128,4,128]{4,3,2,1,0:T(4,128)(2,1)S(1)} %get-tuple-element.33, bf16[1,16,128,4,128]{4,3,2,1,0:T(4,128)(2,1)} %get-tuple-element.34), kind=kLoop, calls=%fused_computation.2 | loop fusion | flops 2097152 | bytes 8388608 | tf_op jit(solution)/shard_map/stack | solution.py:82
  463.3 48.4 %all-reduce.24.cloned.1.call-done = bf16[64,1024]{1,0:T(8,128)(2,1)} async-done(((bf16[64,1024]{1,0:T(8,128)(2,1)}), bf16[64,1024]{1,0:T(8,128)(2,1)}) %all-reduce.24.cloned.1.call-update) | async-done | bytes 131088 | tf_op jit(solution)/shard_map/psum | solution.py:80
  511.7 1.6 fusion.73
  (84 shorter events, 2.3 us)
Async XLA Ops:
  7.2 59.5 %all-reduce.28.cloned.1.call-start = ((), (), s32[]{:S(2)}) async-start(), calls=%async_computation.7 | async-start | bytes 393216 | tf_op jit(solution)/shard_map/psum | solution.py:62
  20.9 3.4 copy-start
  24.3 1.7 copy-start.2
  26.0 1.9 copy-start.1
  27.9 2.8 copy-start.20
  27.9 3.0 copy-start.18
  27.9 3.1 copy-start.9
  29.6 2.2 copy-start.19
  30.6 124.5 %all-reduce.14.cloned.1.call-start = ((), (), s32[]{:S(2)}) async-start(), calls=%async_computation | async-start | bytes 262144 | tf_op jit(solution)/shard_map/psum | solution.py:73
  31.0 48.1 %copy-start.10 = (pred[16,128]{0,1:T(8,128)(4,1)}, pred[16,128]{0,1:T(8,128)(4,1)S(1)}, u32[]{:S(2)}) copy-start(pred[16,128]{0,1:T(8,128)(4,1)S(1)} %copy.38) | copy-start | bytes 6148
  68.4 13.0 %copy-start.12 = (bf16[16,4,128]{2,1,0:T(4,128)(2,1)}, bf16[16,4,128]{2,1,0:T(4,128)(2,1)S(1)}, u32[]{:S(2)}) copy-start(bf16[16,4,128]{2,1,0:T(4,128)(2,1)S(1)} %copy.45) | copy-start | bytes 49156
  68.5 3.6 copy-start.14
  87.1 9.7 %copy-start.21 = (bf16[2,4,128,1024]{3,2,1,0:T(8,128)(2,1)S(1)}, bf16[2,4,128,1024]{3,2,1,0:T(8,128)(2,1)}, u32[]{:S(2)}) copy-start(bf16[2,4,128,1024]{3,2,1,0:T(8,128)(2,1)} %param.26) | copy-start | bytes 6291460
  87.1 10.8 %copy-start.16 = (bf16[2,1024]{1,0:T(2,128)(2,1)S(1)}, bf16[2,1024]{1,0:T(2,128)(2,1)}, u32[]{:S(2)}) copy-start(bf16[2,1024]{1,0:T(2,128)(2,1)} %param.27) | copy-start | bytes 12292
  97.8 106.7 %all-reduce.16.cloned.1.call-start = ((), (), s32[]{:S(2)}) async-start(), calls=%async_computation.1 | async-start | bytes 524288 | tf_op jit(solution)/shard_map/psum | solution.py:77
  168.7 94.7 %copy-start.6 = (bf16[64,1024]{1,0:T(8,128)(2,1)S(1)}, bf16[64,1024]{1,0:T(8,128)(2,1)}, u32[]{:S(2)}) copy-start(bf16[64,1024]{1,0:T(8,128)(2,1)} %all-reduce.14.cloned.1.call-done) | copy-start | bytes 393220
  168.7 105.0 %copy-start.4 = (bf16[1,1024,4,128]{3,2,1,0:T(4,128)(2,1)S(1)}, bf16[1,1024,4,128]{3,2,1,0:T(4,128)(2,1)}, u32[]{:S(2)}) copy-start(bf16[1,1024,4,128]{3,2,1,0:T(4,128)(2,1)} %get-tuple-element.23) | copy-start | bytes 3145732
  168.7 94.7 %all-reduce.18.cloned.1.call-start = ((), (), s32[]{:S(2)}) async-start(), calls=%async_computation.2 | async-start | bytes 262144 | tf_op jit(solution)/shard_map/psum | solution.py:80
  208.2 67.1 %copy-start.5 = (bf16[1,1024,4,128]{3,2,1,0:T(4,128)(2,1)S(1)}, bf16[1,1024,4,128]{3,2,1,0:T(4,128)(2,1)}, u32[]{:S(2)}) copy-start(bf16[1,1024,4,128]{3,2,1,0:T(4,128)(2,1)} %get-tuple-element.21) | copy-start | bytes 3145732
  208.2 68.8 %copy-start.3 = (bf16[1,1024,4,128]{3,2,1,0:T(4,128)(2,1)S(1)}, bf16[1,1024,4,128]{3,2,1,0:T(4,128)(2,1)}, u32[]{:S(2)}) copy-start(bf16[1,1024,4,128]{3,2,1,0:T(4,128)(2,1)} %get-tuple-element.26) | copy-start | bytes 3145732
  208.3 106.1 %all-reduce.26.cloned.1.call-start = ((), (), s32[]{:S(2)}) async-start(), calls=%async_computation.6 | async-start | bytes 393216 | tf_op jit(solution)/shard_map/psum | solution.py:62
  273.7 40.7 %copy-start.7 = (bf16[1,128,4,128]{3,2,1,0:T(4,128)(2,1)S(1)}, bf16[1,128,4,128]{3,2,1,0:T(4,128)(2,1)}, u32[]{:S(2)}) copy-start(bf16[1,128,4,128]{3,2,1,0:T(4,128)(2,1)} %get-tuple-element.28) | copy-start | bytes 393220
  278.7 124.7 %all-reduce.20.cloned.1.call-start = ((), (), s32[]{:S(2)}) async-start(), calls=%async_computation.3 | async-start | bytes 262144 | tf_op jit(solution)/shard_map/psum | solution.py:73
  318.2 9.2 %copy-start.11 = (pred[16,128]{0,1:T(8,128)(4,1)S(1)}, pred[16,128]{0,1:T(8,128)(4,1)}, u32[]{:S(2)}) copy-start(pred[16,128]{0,1:T(8,128)(4,1)} %copy-done.10) | copy-start | bytes 6148
  335.4 9.7 %copy-start.22 = (bf16[2,4,128,1024]{3,2,1,0:T(8,128)(2,1)S(1)}, bf16[2,4,128,1024]{3,2,1,0:T(8,128)(2,1)}, u32[]{:S(2)}) copy-start(bf16[2,4,128,1024]{3,2,1,0:T(8,128)(2,1)} %param.26) | copy-start | bytes 6291460
  335.4 10.8 %copy-start.13 = (bf16[16,4,128]{2,1,0:T(4,128)(2,1)S(1)}, bf16[16,4,128]{2,1,0:T(4,128)(2,1)}, u32[]{:S(2)}) copy-start(bf16[16,4,128]{2,1,0:T(4,128)(2,1)} %copy-done.12) | copy-start | bytes 49156
  335.4 10.8 %copy-start.15 = (bf16[16,4,128]{2,1,0:T(4,128)(2,1)S(1)}, bf16[16,4,128]{2,1,0:T(4,128)(2,1)}, u32[]{:S(2)}) copy-start(bf16[16,4,128]{2,1,0:T(4,128)(2,1)} %copy-done.14) | copy-start | bytes 49156
  346.1 66.9 %copy-start.17 = (f32[1,1024]{1,0:T(1,128)S(1)}, f32[1,1024]{1,0:T(1,128)}, u32[]{:S(2)}) copy-start(f32[1,1024]{1,0:T(1,128)} %get-tuple-element.32) | copy-start | bytes 12292
  346.1 106.6 %all-reduce.22.cloned.1.call-start = ((), (), s32[]{:S(2)}) async-start(), calls=%async_computation.4 | async-start | bytes 524288 | tf_op jit(solution)/shard_map/psum | solution.py:77
  417.0 94.7 %all-reduce.24.cloned.1.call-start = ((), (), s32[]{:S(2)}) async-start(), calls=%async_computation.5 | async-start | bytes 262144 | tf_op jit(solution)/shard_map/psum | solution.py:80
  456.5 55.2 %copy-start.8 = (bf16[64,1024]{1,0:T(8,128)(2,1)S(1)}, bf16[64,1024]{1,0:T(8,128)(2,1)}, u32[]{:S(2)}) copy-start(bf16[64,1024]{1,0:T(8,128)(2,1)} %all-reduce.20.cloned.1.call-done) | copy-start | bytes 393220
Sparse Core Ops, SparseCore 0:
  30.8 35.9 all-reduce.27
  97.9 57.2 all-reduce.13
  168.8 35.5 all-reduce.15
  208.4 54.9 all-reduce.17
  278.8 35.4 all-reduce.25
  346.2 57.1 all-reduce.19
  417.1 35.5 all-reduce.21
  456.7 54.9 all-reduce.23
where the time goes:
time: 523 us; the launch traced here: 520 us
  waiting for transfers between devices  342 us (65%)
  other arithmetic  62.7 us (12%)
  blocking collectives  54.9 us (10%)
  matrix products  28.1 us (5%)
  local copies, waits for them, and re-layouts  16.8 us (3%)
  between operations  14.5 us (3%)
    psum x2, waiting for transfers between devices, local_step(): attn_out = lax.psum(attn_part, 'x')  104 us
    psum x2, waiting for transfers between devices, local_step(): down_out = lax.psum(down_part, 'x')  103 us
    psum x2, waiting for transfers between devices, local_step(): q_full, k_full, v_full = lax.psum((q_part, k_part, v_part), 'y')  70.5 us
    psum x2, waiting for transfers between devices, local_step(): up_proj = lax.psum(up_part, 'y')  63.7 us
    psum x4, blocking collectives, sharded_norm(): lax.psum(jnp.sum(hidden_wide * hidden_wide, axis=1, keepdims=True), 'y')  36.9 us
    select_n x3, other arithmetic, write_rows(): jnp.where(hit_mask[:, :, None, None], new_rows[:, None, :, :], cache_layer)  20.9 us
    all_gather x2, blocking collectives, local_step(): context_all = lax.all_gather(context, 'y', axis=0, tiled=True)  18 us
    unnamed x4, other arithmetic  15.7 us
  transfers between devices with their start and end apart: 8, of which 8 were waited for; matrix products, arithmetic and copies ran while one was open for 5% of the time, Pallas kernels for 0%

commit v1 on v0

v1 whole, which is shorter than its diff:
```python
import functools

import jax
import jax.numpy as jnp
from jax import lax
from jax.experimental import pallas as pl
from jax.experimental.pallas import tpu as pltpu
from jax.sharding import PartitionSpec as P

EPS = 1e-6
F32 = jnp.float32
BF16 = jnp.bfloat16
MESH = pl.DeviceIdType.MESH


def step_kernel(dims, hidden_in, len_in, kc_in, vc_in, rel_in, na_in, wq_in, wk_in, wv_in, bu_in, bw_in, wo_in, nm_in, wup_in, wdn_in,
                hid_out, kn_out, vn_out,
                hid_v, len_v, kc_v, vc_v, rel_v, na_v, nm_v, bu_v, bw_v, wraw_v, wqkv_v, wo_v, wup_v, wdn_v,
                wtmp, relf_v, r0_v, h_v, a_s, c_s, k_s, v_s, ctx_s, kn_v, vn_v, acc_v, outh_v,
                ss_rx, qkv_tx, qkv_rx, ctx_all, rs_tx, rs_rx, xg, up_tx, up_rx, act,
                ld_sem, out_sem, ss_ss, ss_rs, qkv_ss, qkv_rs, ctx_ss, ctx_rs, rs_ss, rs_rs, ag_ss, ag_rs, up_ss, up_rs, act_ss, act_rs):
    layers, ny, nx, rows, heads, hd, seq, d_loc, ff_loc = dims
    d_total = d_loc * ny
    rb = rows // ny
    hh = heads * hd
    cb = d_loc // nx
    fb = ff_loc // ny
    cells = rb * heads
    kl = seq * heads
    chips = nx // 2
    my = lax.axis_index("y")
    mx = lax.axis_index("x")
    my_chip = mx // 2
    my_core = lax.rem(mx, 2)
    partner = 2 * my_chip + 1 - my_core

    barrier = pltpu.get_barrier_semaphore()
    for d in range(1, ny):
        pl.semaphore_signal(barrier, inc=1, device_id={"y": lax.rem(my + d, ny)}, device_id_type=MESH)
    for d in range(1, nx):
        pl.semaphore_signal(barrier, inc=1, device_id={"x": lax.rem(mx + d, nx)}, device_id_type=MESH)

    loads = {}

    def load(name, src, dst):
        c = pltpu.make_async_copy(src, dst, ld_sem.at[len(loads)])
        c.start()
        loads[name] = c

    load("hid", hidden_in, hid_v)
    load("na", na_in, na_v)
    for j, w in enumerate((wq_in, wk_in, wv_in)):
        load(("w", 0, j), w.at[0], wraw_v.at[0, j])
    load("len", len_in, len_v)
    load("rel", rel_in, rel_v)
    load("bu", bu_in, bu_v)
    load("bw", bw_in, bw_v)
    load("nm", nm_in, nm_v)
    load(("k", 0), kc_in.at[0], kc_v.at[0])
    load(("v", 0), vc_in.at[0], vc_v.at[0])
    load(("o", 0), wo_in.at[0], wo_v.at[0])
    load(("up", 0), wup_in.at[0], wup_v.at[0])
    load(("dn", 0), wdn_in.at[0], wdn_v.at[0])
    for l in range(1, layers):
        for j, w in enumerate((wq_in, wk_in, wv_in)):
            load(("w", l, j), w.at[l], wraw_v.at[l, j])
        load(("k", l), kc_in.at[l], kc_v.at[l])
        load(("v", l), vc_in.at[l], vc_v.at[l])
        load(("o", l), wo_in.at[l], wo_v.at[l])
        load(("up", l), wup_in.at[l], wup_v.at[l])
        load(("dn", l), wdn_in.at[l], wdn_v.at[l])

    sends = []

    def send(src, dst, ss, rs, dev):
        c = pltpu.make_async_remote_copy(src_ref=src, dst_ref=dst, send_sem=ss, recv_sem=rs, device_id=dev, device_id_type=MESH)
        c.start()
        sends.append(c)

    def recv(dst, ss, rs, dev):
        pltpu.make_async_remote_copy(src_ref=dst, dst_ref=dst, send_sem=ss, recv_sem=rs, device_id=dev, device_id_type=MESH).wait_recv()

    y_order = [2, 1, 3] if ny == 4 else list(range(1, ny))
    chunk_k = 128
    chunk = chunk_k * heads

    def relayout(l, j):
        def body(i, carry):
            wtmp[...] = wraw_v[l, j, pl.ds(pl.multiple_of(i * chunk, chunk), chunk), :].astype(F32)
            for h in range(heads):
                wqkv_v[l, pl.ds(pl.multiple_of(i * chunk_k, chunk_k), chunk_k), j * hh + h * hd:j * hh + (h + 1) * hd] = wtmp[pl.ds(h, chunk_k, stride=heads), :].astype(BF16)
            return carry
        lax.fori_loop(0, d_loc // chunk_k, body, 0)

    lane = lax.broadcasted_iota(jnp.int32, (rows, 128), 1)
    rown = lax.broadcasted_iota(jnp.int32, (rows, 128), 0)
    diag = lane == rown

    def norm_stage(n, p, gain):
        blocks = [xg[p, j].astype(F32) for j in range(nx)]
        sq = blocks[0] * blocks[0]
        for j in range(1, nx):
            sq = sq + blocks[j] * blocks[j]
        ssq = jnp.sum(sq, axis=1, keepdims=True)
        row = jnp.sum(jnp.where(diag, ssq, 0.0), axis=0, keepdims=True)
        ss_rx[n, my] = jnp.broadcast_to(row, (8, 128))
        for d in y_order:
            peer = lax.rem(my + d, ny)
            send(ss_rx.at[n, my], ss_rx.at[n, my], ss_ss.at[n, peer], ss_rs.at[n, my], {"y": peer})
        inv = lax.rsqrt(ssq / d_loc + EPS)
        for j in range(nx):
            h_v[:, j * cb:(j + 1) * cb] = (blocks[j] * inv * gain[:, j * cb:(j + 1) * cb].astype(F32)).astype(BF16)

    def ratio_rows(n):
        for d in y_order:
            src = lax.rem(my + d, ny)
            recv(ss_rx.at[n, src], ss_ss.at[n, src], ss_rs.at[n, src], {"y": src})
        parts = [ss_rx[n, s][0:1] for s in range(ny)]
        total = parts[0]
        for s in range(1, ny):
            total = total + parts[s]
        inv = lax.rsqrt(total / d_total + EPS)
        finite = total < jnp.inf
        return [jnp.where(finite, inv * jnp.sqrt(parts[s] / d_loc + EPS), 0.0) for s in range(ny)]

    def to_column(row, index):
        return jnp.sum(jnp.where(lax.broadcasted_iota(jnp.int32, index.shape, 1) == index, row, 0.0), axis=1, keepdims=True)

    def x_reduce(p, matmul):
        for dc in ([2, 1, 3, 0] if chips == 4 else list(range(1, chips)) + [0]):
            chip = lax.rem(my_chip + dc, chips)
            part = matmul(pl.multiple_of(chip * 2 * cb, 2 * cb)).astype(BF16)
            rs_tx[p, 2 * chip] = part[:, :cb]
            rs_tx[p, 2 * chip + 1] = part[:, cb:]
            if dc:
                for core in range(2):
                    dst = 2 * chip + core
                    send(rs_tx.at[p, dst], rs_rx.at[p, mx], rs_ss.at[p, dst], rs_rs.at[p, mx], {"x": dst})
            else:
                send(rs_tx.at[p, partner], rs_rx.at[p, mx], rs_ss.at[p, partner], rs_rs.at[p, mx], {"x": partner})
        total = rs_tx[p, mx].astype(F32)
        for d in [nx - d for d in range(1, nx)]:
            src = lax.rem(mx + d, nx)
            recv(rs_rx.at[p, src], rs_ss.at[p, src], rs_rs.at[p, src], {"x": src})
            total = total + rs_rx[p, src].astype(F32)
        xg[p + 1, mx] = (xg[p, mx].astype(F32) + total).astype(BF16)
        for d in [4, 3, 5, 2, 6, 1, 7]:
            dst = lax.rem(mx + d, nx)
            send(xg.at[p + 1, mx], xg.at[p + 1, mx], ag_ss.at[p, dst], ag_rs.at[p, mx], {"x": dst})

    def x_gather_wait(p):
        for d in range(1, nx):
            src = lax.rem(mx + d, nx)
            recv(xg.at[p + 1, src], ag_ss.at[p, src], ag_rs.at[p, src], {"x": src})

    loads["hid"].wait()
    for j in range(nx):
        xg[0, j] = hid_v[:, j * cb:(j + 1) * cb]
    for j in range(3):
        loads["w", 0, j].wait()
        relayout(0, j)
    loads["na"].wait()
    loads["len"].wait()
    loads["rel"].wait()
    loads["bu"].wait()
    loads["bw"].wait()
    loads["nm"].wait()
    pl.semaphore_wait(barrier, ny - 1 + nx - 1)

    cell_row = lax.broadcasted_iota(jnp.int32, (cells, 1), 0)
    key_lane = lax.broadcasted_iota(jnp.int32, (cells, kl), 1)
    key_row = lax.broadcasted_iota(jnp.int32, (cells, kl), 0)
    group_row = lax.broadcasted_iota(jnp.int32, (16, 1), 0) // heads
    per_group = 16 // heads

    def prepare_rel(l):
        pr = lax.broadcasted_iota(jnp.int32, (kl, kl), 0)
        pc = lax.broadcasted_iota(jnp.int32, (kl, kl), 1)
        flip = (pc == (seq - 1 - pr // heads) * heads + lax.rem(pr, heads)).astype(F32).astype(BF16)
        relf_v[l] = jnp.dot(flip, rel_v[l], preferred_element_type=F32).astype(BF16)
        first = rel_v[l, 0:16].astype(F32)
        for h in range(heads):
            r0_v[l, pl.ds(h, rb, stride=heads), :] = jnp.broadcast_to(first[h:h + 1], (rb, hd))

    for l in range(layers):
        p = 2 * l
        norm_stage(2 * l, p, na_v[l:l + 1])
        for j in range(3):
            part = jnp.dot(h_v[...], wqkv_v[l, :, j * hh:(j + 1) * hh], preferred_element_type=F32)
            qkv_tx[l, j] = part.astype(BF16)
            for d in y_order:
                peer = lax.rem(my + d, ny)
                rows_at = pl.multiple_of(peer * rb, rb)
                send(qkv_tx.at[l, j, pl.ds(rows_at, rb)], qkv_rx.at[l, my, j], qkv_ss.at[l, j, peer], qkv_rs.at[l, j, my], {"y": peer})
        own_at = pl.multiple_of(my * rb, rb)
        for j in range(3):
            qkv_rx[l, my, j] = qkv_tx[l, j, pl.ds(own_at, rb), :]
        if l == 0:
            for l2 in range(layers):
                prepare_rel(l2)
            for l2 in range(1, layers):
                for j in range(3):
                    loads["w", l2, j].wait()
                    relayout(l2, j)
        lens_row = len_v[...].astype(F32)
        want = my * rb + lax.broadcasted_iota(jnp.int32, (cells, rows), 0) // heads
        lens = to_column(lens_row, want).astype(jnp.int32)
        ratios = ratio_rows(2 * l)
        want16 = my * rb + lax.broadcasted_iota(jnp.int32, (rb, 128), 0)
        cols = [to_column(r, want16) for r in ratios]

        def gathered(j):
            for d in y_order:
                src = lax.rem(my + d, ny)
                recv(qkv_rx.at[l, src, j], qkv_ss.at[l, j, src], qkv_rs.at[l, j, src], {"y": src})
            tot = qkv_rx[l, 0, j].astype(F32) * cols[0]
            for s in range(1, ny):
                tot = tot + qkv_rx[l, s, j].astype(F32) * cols[s]
            return tot.astype(BF16).astype(F32)

        q = gathered(0)
        for h in range(heads):
            qh = q[:, h * hd:(h + 1) * hd]
            a_s[pl.ds(h, rb, stride=heads), :] = qh + bu_v[l, h:h + 1].astype(F32)
            c_s[pl.ds(h, rb, stride=heads), :] = qh + bw_v[l, h:h + 1].astype(F32)
        a = a_s[...].astype(BF16)
        c = c_s[...].astype(BF16)
        rel = lax.dot_general(c, relf_v[l], (((1,), (1,)), ((), ())), preferred_element_type=F32)
        shift = seq - 1 - lens
        bit = 1
        while bit < seq:
            rolled = pltpu.roll(rel, kl - bit * heads, 1)
            rel = jnp.where(lax.rem(shift // bit, 2) == 1, rolled, rel)
            bit *= 2
        loads["k", l].wait()
        score_parts = []
        for g in range(cells // 16):
            ag = a[16 * g:16 * g + 16]
            sg = None
            for i in range(per_group):
                o = lax.dot_general(ag, kc_v[l, g * per_group + i], (((1,), (1,)), ((), ())), preferred_element_type=F32)
                sg = o if sg is None else jnp.where(group_row == i, o, sg)
            score_parts.append(sg)
        scores = jnp.concatenate(score_parts, axis=0)
        k = gathered(1)
        v = gathered(2)
        for h in range(heads):
            k_s[pl.ds(h, rb, stride=heads), :] = k[:, h * hd:(h + 1) * hd]
            v_s[pl.ds(h, rb, stride=heads), :] = v[:, h * hd:(h + 1) * hd]
        kn = k_s[...]
        vn = v_s[...]
        kn_v[l] = kn.astype(BF16)
        vn_v[l] = vn.astype(BF16)
        scale = hd ** -0.5
        s_new = (jnp.sum(a.astype(F32) * kn, axis=1, keepdims=True) + jnp.sum(c.astype(F32) * r0_v[l], axis=1, keepdims=True)) * scale
        valid = (lax.rem(key_lane, heads) == lax.rem(key_row, heads)) & (key_lane // heads < lens)
        scores = jnp.where(valid, (scores + rel) * scale, -jnp.inf)
        top = jnp.maximum(jnp.max(scores, axis=1, keepdims=True), s_new)
        e = jnp.exp(scores - top)
        e_new = jnp.exp(s_new - top)
        inv_den = 1.0 / (jnp.sum(e, axis=1, keepdims=True) + e_new)
        prob = (e * inv_den).astype(BF16)
        p_new = (e_new * inv_den).astype(BF16).astype(F32)
        loads["v", l].wait()
        ctx_parts = []
        for g in range(cells // 16):
            pg = prob[16 * g:16 * g + 16]
            cg = None
            for i in range(0, per_group, 2):
                b = g * per_group + i
                pair = jnp.concatenate([vc_v[l, b], vc_v[l, b + 1]], axis=1)
                o = jnp.dot(pg, pair, preferred_element_type=F32)
                cg = o[:, :hd] if cg is None else jnp.where(group_row == i, o[:, :hd], cg)
                cg = jnp.where(group_row == i + 1, o[:, hd:], cg)
            ctx_parts.append(cg)
        ctx_s[...] = jnp.concatenate(ctx_parts, axis=0) + p_new * vn
        for h in range(heads):
            ctx_all[l, my, :, h * hd:(h + 1) * hd] = ctx_s[pl.ds(h, rb, stride=heads), :].astype(BF16)
        for d in y_order:
            peer = lax.rem(my + d, ny)
            send(ctx_all.at[l, my], ctx_all.at[l, my], ctx_ss.at[l, peer], ctx_rs.at[l, my], {"y": peer})
        loads["o", l].wait()
        for d in y_order:
            src = lax.rem(my + d, ny)
            recv(ctx_all.at[l, src], ctx_ss.at[l, src], ctx_rs.at[l, src], {"y": src})
        ctx = jnp.concatenate([ctx_all[l, s] for s in range(ny)], axis=0)
        x_reduce(p, lambda at: jnp.dot(ctx, wo_v[l, :, pl.ds(at, 2 * cb)], preferred_element_type=F32))
        x_gather_wait(p)
        p = 2 * l + 1
        norm_stage(p, p, nm_v[l:l + 1])
        loads["up", l].wait()
        for d in y_order + [0]:
            dst = lax.rem(my + d, ny)
            part = jnp.dot(h_v[...], wup_v[l, :, pl.ds(pl.multiple_of(dst * fb, fb), fb)], preferred_element_type=F32).astype(BF16)
            if d:
                up_tx[l, dst] = part
                send(up_tx.at[l, dst], up_rx.at[l, my], up_ss.at[l, dst], up_rs.at[l, my], {"y": dst})
            else:
                up_rx[l, my] = part
        ratios = ratio_rows(p)
        cols = [to_column(r, rown) for r in ratios]
        for d in y_order:
            src = lax.rem(my + d, ny)
            recv(up_rx.at[l, src], up_ss.at[l, src], up_rs.at[l, src], {"y": src})
        tot = up_rx[l, 0].astype(F32) * cols[0]
        for s in range(1, ny):
            tot = tot + up_rx[l, s].astype(F32) * cols[s]
        act[l, my] = jax.nn.gelu(tot.astype(BF16).astype(F32), approximate=True).astype(BF16)
        for d in y_order:
            peer = lax.rem(my + d, ny)
            send(act.at[l, my], act.at[l, my], act_ss.at[l, peer], act_rs.at[l, my], {"y": peer})
        loads["dn", l].wait()

        def down_rows(src):
            return pl.ds(pl.multiple_of(src * fb, fb), fb)

        acc_v[...] = jnp.dot(act[l, my], wdn_v[l, down_rows(my), :], preferred_element_type=F32)
        for d in reversed(y_order[1:]):
            src = lax.rem(my + d, ny)
            recv(act.at[l, src], act_ss.at[l, src], act_rs.at[l, src], {"y": src})
            acc_v[...] += jnp.dot(act[l, src], wdn_v[l, down_rows(src), :], preferred_element_type=F32)
        src = lax.rem(my + y_order[0], ny)
        recv(act.at[l, src], act_ss.at[l, src], act_rs.at[l, src], {"y": src})
        x_reduce(p, lambda at: acc_v[:, pl.ds(at, 2 * cb)] + jnp.dot(act[l, src], wdn_v[l, down_rows(src), pl.ds(at, 2 * cb)], preferred_element_type=F32))
        x_gather_wait(p)

    last = 2 * layers
    for j in range(nx):
        outh_v[:, j * cb:(j + 1) * cb] = xg[last, j]
    outs = [pltpu.make_async_copy(outh_v, hid_out, out_sem.at[0]),
            pltpu.make_async_copy(kn_v, kn_out, out_sem.at[1]),
            pltpu.make_async_copy(vn_v, vn_out, out_sem.at[2])]
    for o in outs:
        o.start()
    for c in sends:
        c.wait_send()
    for o in outs:
        o.wait()


def cache_kernel(dims, len_ref, hid_in, kc_in, vc_in, kn_in, vn_in, hid_out, kc_out, vc_out, hid_v, kc_v, vc_v, kn_v, vn_v, in_sem, out_sem):
    layers, rb = dims
    my = lax.axis_index("y")
    ins = []
    for i, (src, dst) in enumerate(((kn_in, kn_v), (vn_in, vn_v), (hid_in, hid_v))):
        c = pltpu.make_async_copy(src, dst, in_sem.at[i])
        c.start()
        ins.append(c)
    half = rb // 2
    parts = []
    for l in range(layers):
        for src, buf, new, dst in ((kc_in, kc_v, kn_v, kc_out), (vc_in, vc_v, vn_v, vc_out)):
            for s in range(2):
                at = pl.ds(s * half, half)
                i = len(parts)
                r = pltpu.make_async_copy(src.at[l, at], buf.at[l, at], in_sem.at[3 + i])
                r.start()
                parts.append((r, pltpu.make_async_copy(buf.at[l, at], dst.at[l, at], out_sem.at[1 + i]), buf, new, l, s * half))
    for c in ins:
        c.wait()
    out_h = pltpu.make_async_copy(hid_v, hid_out, out_sem.at[0])
    out_h.start()
    for r, w, buf, new, l, b0 in parts:
        r.wait()
        for b in range(b0, b0 + half):
            buf[l, b, len_ref[my * rb + b]] = new[l, b]
        w.start()
    out_h.wait()
    for part in parts:
        part[1].wait()


def solution(mesh):
    ny = mesh.shape["y"]
    nx = mesh.shape["x"]
    cache_spec = P(None, ("rep", "y"), None, "x", None)
    row_spec = P("rep", "y")
    proj_spec = P(None, "y", "x", None)
    head_spec = P(None, "x", None)
    in_specs = (row_spec, P("rep"), cache_spec, cache_spec, P(None, None, "x", None), P(None, "y"),
                proj_spec, proj_spec, proj_spec, head_spec, head_spec, P(None, "x", None, "y"),
                P(None, "y"), P(None, "y", "x"), P(None, "x", "y"))
    out_specs = (row_spec, cache_spec, cache_spec)

    def local_step(hidden, lengths, k_cache, v_cache, rel_table, norm_attn, w_q, w_k, w_v, bias_content, bias_pos, w_out, norm_mlp, w_up, w_down):
        layers, rb, seq, heads, hd = k_cache.shape
        rows, d_loc = hidden.shape
        ff_loc = w_up.shape[2]
        hh = heads * hd
        cells = rb * heads
        kl = seq * heads
        cb = d_loc // nx
        fb = ff_loc // ny
        dims = (layers, ny, nx, rows, heads, hd, seq, d_loc, ff_loc)
        any_spec = pl.BlockSpec(memory_space=pl.ANY)
        vmem = pltpu.VMEM
        dma = pltpu.SemaphoreType.DMA
        scratch = [
            vmem((rows, d_loc), BF16), vmem((1, rows), jnp.int32),
            vmem((layers, rb, kl, hd), BF16), vmem((layers, rb, kl, hd), BF16),
            vmem((layers, kl, hd), BF16), vmem((layers, d_loc), BF16), vmem((layers, d_loc), BF16),
            vmem((layers, heads, hd), BF16), vmem((layers, heads, hd), BF16),
            vmem((layers, 3, d_loc * heads, hd), BF16), vmem((layers, d_loc, 3 * hh), BF16),
            vmem((layers, hh, d_loc), BF16), vmem((layers, d_loc, ff_loc), BF16), vmem((layers, ff_loc, d_loc), BF16),
            vmem((128 * heads, hd), F32), vmem((layers, kl, hd), BF16), vmem((layers, cells, hd), F32), vmem((rows, d_loc), BF16),
            vmem((cells, hd), F32), vmem((cells, hd), F32), vmem((cells, hd), F32), vmem((cells, hd), F32), vmem((cells, hd), F32),
            vmem((layers, cells, hd), BF16), vmem((layers, cells, hd), BF16), vmem((rows, d_loc), F32), vmem((rows, d_loc), BF16),
            vmem((2 * layers, ny, 8, 128), F32),
            vmem((layers, 3, rows, hh), BF16), vmem((layers, ny, 3, rb, hh), BF16), vmem((layers, ny, rb, hh), BF16),
            vmem((2 * layers, nx, rows, cb), BF16), vmem((2 * layers, nx, rows, cb), BF16), vmem((2 * layers + 1, nx, rows, cb), BF16),
            vmem((layers, ny, rows, fb), BF16), vmem((layers, ny, rows, fb), BF16), vmem((layers, ny, rows, fb), BF16),
            dma((7 + 8 * layers,)), dma((3,)),
            dma((2 * layers, ny)), dma((2 * layers, ny)), dma((layers, 3, ny)), dma((layers, 3, ny)),
            dma((layers, ny)), dma((layers, ny)), dma((2 * layers, nx)), dma((2 * layers, nx)),
            dma((2 * layers, nx)), dma((2 * layers, nx)), dma((layers, ny)), dma((layers, ny)), dma((layers, ny)), dma((layers, ny)),
        ]
        new_shape = jax.ShapeDtypeStruct((layers, cells, hd), BF16)
        hid, k_new, v_new = pl.pallas_call(
            functools.partial(step_kernel, dims),
            out_shape=(jax.ShapeDtypeStruct((rows, d_loc), BF16), new_shape, new_shape),
            in_specs=[any_spec] * 15,
            out_specs=(any_spec,) * 3,
            scratch_shapes=scratch,
            compiler_params=pltpu.CompilerParams(collective_id=0, has_side_effects=True, vmem_limit_bytes=67043328),
            name="decode_step",
        )(hidden, lengths.reshape(1, rows), k_cache.reshape(layers, rb, kl, hd), v_cache.reshape(layers, rb, kl, hd),
          rel_table.reshape(layers, kl, hd), norm_attn,
          w_q.reshape(layers, d_loc * heads, hd), w_k.reshape(layers, d_loc * heads, hd), w_v.reshape(layers, d_loc * heads, hd),
          bias_content, bias_pos, w_out.reshape(layers, hh, d_loc), norm_mlp, w_up, w_down)

        cache_shape = jax.ShapeDtypeStruct(k_cache.shape, BF16)
        return pl.pallas_call(
            functools.partial(cache_kernel, (layers, rb)),
            out_shape=(jax.ShapeDtypeStruct((rows, d_loc), BF16), cache_shape, cache_shape),
            in_specs=[pl.BlockSpec(memory_space=pltpu.SMEM)] + [any_spec] * 5,
            out_specs=(any_spec,) * 3,
            scratch_shapes=[
                vmem((rows, d_loc), BF16), vmem(k_cache.shape, BF16), vmem(k_cache.shape, BF16),
                vmem((layers, rb, heads, hd), BF16), vmem((layers, rb, heads, hd), BF16),
                dma((3 + 4 * layers,)), dma((1 + 4 * layers,)),
            ],
            name="cache_write",
        )(lengths, hid, k_cache, v_cache, k_new.reshape(layers, rb, heads, hd), v_new.reshape(layers, rb, heads, hd))

    return jax.shard_map(local_step, mesh=mesh, in_specs=in_specs, out_specs=out_specs, check_vma=False)
```

time: 523 us -> 93.2 us (0.18)
  waiting for transfers between devices: 342 us -> 0 us
  Pallas kernels: 0 us -> 92.5 us
  other arithmetic: 62.7 us -> 0 us
  blocking collectives: 54.9 us -> 0 us
  matrix products: 28.1 us -> 0 us
  local copies, waits for them, and re-layouts: 16.8 us -> 0 us
  between operations: 14.5 us -> 0.64 us
    psum x8 -> x0, waiting for transfers between devices: 342 us -> none  [the longest x2 104 us: local_step(): attn_out = lax.psum(attn_part, 'x')]
    pallas_call x0 -> x2, Pallas kernels: none -> 92.5 us  [the longest x1 85.2 us: local_step(): pl.pallas_call(functools.partial(step_kernel, dims), out_shape=(jax.Shape...]
    psum x4 -> x0, blocking collectives: 36.9 us -> none  [sharded_norm(): lax.psum(jnp.sum(hidden_wide * hidden_wide, axis=1, keepdims=True), 'y')]
    dot_general x16 -> x0, matrix products: 28.1 us -> none  [the longest x2 7.76 us: local_step(): jnp.dot(normed, w_up[layer], preferred_element_type=jnp.float32)]
    select_n x3 -> x0, other arithmetic: 20.9 us -> none  [write_rows(): jnp.where(hit_mask[:, :, None, None], new_rows[:, None, :, :], cache_layer)]
    all_gather x2 -> x0, blocking collectives: 18 us -> none  [local_step(): context_all = lax.all_gather(context, 'y', axis=0, tiled=True)]
    unnamed x4 -> x0, other arithmetic: 15.7 us -> none
    another operation x2 -> x0, other arithmetic: 14.2 us -> none  [local_step(): return (hidden, jnp.stack(k_layers), jnp.stack(v_layers))]
  transfers between devices with their start and end apart: 8 -> 0, of which waited for: 8 -> 0; matrix products, arithmetic and copies ran while one was open for 5% -> 0% of each run, Pallas kernels for 0% -> 0%
where the time goes in v1:
time: 93.2 us; the launch traced here: 93.1 us
  Pallas kernels  92.5 us (99%)
    pallas_call x1, Pallas kernels, local_step(): pl.pallas_call(functools.partial(step_kernel, dims), out_shape=(jax.Shape...  85.2 us
    pallas_call x1, Pallas kernels, local_step(): pl.pallas_call(functools.partial(cache_kernel, (layers, rb)), out_shape=(...  7.32 us

profile of v1, /device:TPU:97, one launch (start us, length us, event | category | flops | bytes accessed | tf_op | source)
XLA Modules:
  0.0 93.1 jit_solution(14151127373362160750)
XLA Ops:
  0.6 85.2 %decode_step.1 = (bf16[64,1024]{1,0:T(8,128)(2,1)}, bf16[2,64,128]{2,1,0:T(8,128)(2,1)}, bf16[2,64,128]{2,1,0:T(8,128)(2,1)}) custom-call(bf16[64,1024]{1,0:T(8,128)(2,1)} %hidden_in.1, s32[1,64]{1,0:T(1,128)} %bitcast.19, bf16[2,16,512,128]{3,2,1,0:T(8,128)(2,1)} %bitcast.10, bf16[2,16,512,128]{3,2,1,0:T(8,128)(2,1)} %bitcast.11, ...), custom_call_target="tpu_custom_call" | custom-call | tf_op jit(solution)/shard_map/decode_step/pallas_call | solution.py:418
  85.8 7.3 %cache_write.1 = (bf16[64,1024]{1,0:T(8,128)(2,1)}, bf16[2,16,128,4,128]{4,3,2,1,0:T(4,128)(2,1)}, bf16[2,16,128,4,128]{4,3,2,1,0:T(4,128)(2,1)}) custom-call(s32[64]{0:T(128)} %len_ref.1, bf16[64,1024]{1,0:T(8,128)(2,1)} %get-tuple-element.6.hid_in, bf16[2,16,128,4,128]{4,3,2,1,0:T(4,128)(2,1)} %kc_in.1, bf16[2,16,128,4,128]{4,3,2,1,0:T(4,128)(2,1)} %vc_in.1, ...), custom_call_target="tpu_custom_call" | custom-call | tf_op jit(solution)/shard_map/cache_write/pallas_call | solution.py:432

commit v2 on v1

--- a/solution.py
+++ b/solution.py
@@ -14,11 +14,11 @@
 
 
 def step_kernel(dims, hidden_in, len_in, kc_in, vc_in, rel_in, na_in, wq_in, wk_in, wv_in, bu_in, bw_in, wo_in, nm_in, wup_in, wdn_in,
-                hid_out, kn_out, vn_out,
-                hid_v, len_v, kc_v, vc_v, rel_v, na_v, nm_v, bu_v, bw_v, wraw_v, wqkv_v, wo_v, wup_v, wdn_v,
-                wtmp, relf_v, r0_v, h_v, a_s, c_s, k_s, v_s, ctx_s, kn_v, vn_v, acc_v, outh_v,
+                hid_out, kc_v, vc_v,
+                hid_v, len_v, rel_v, na_v, nm_v, bu_v, bw_v, wraw_v, wqkv_v, wo_v, wup_v, wdn_v,
+                wtmp, relf_v, r0_v, h_v, a_s, c_s, k_s, v_s, ctx_s, acc_v, pos_v, lent_s, kt_s, vt_s,
                 ss_rx, qkv_tx, qkv_rx, ctx_all, rs_tx, rs_rx, xg, up_tx, up_rx, act,
-                ld_sem, out_sem, ss_ss, ss_rs, qkv_ss, qkv_rs, ctx_ss, ctx_rs, rs_ss, rs_rs, ag_ss, ag_rs, up_ss, up_rs, act_ss, act_rs):
+                ld_sem, ss_ss, ss_rs, qkv_ss, qkv_rs, ctx_ss, ctx_rs, rs_ss, rs_rs, ag_ss, ag_rs, up_ss, up_rs, act_ss, act_rs):
     layers, ny, nx, rows, heads, hd, seq, d_loc, ff_loc = dims
     d_total = d_loc * ny
     rb = rows // ny
@@ -27,12 +27,8 @@
     fb = ff_loc // ny
     cells = rb * heads
     kl = seq * heads
-    chips = nx // 2
     my = lax.axis_index("y")
     mx = lax.axis_index("x")
-    my_chip = mx // 2
-    my_core = lax.rem(mx, 2)
-    partner = 2 * my_chip + 1 - my_core
 
     barrier = pltpu.get_barrier_semaphore()
     for d in range(1, ny):
@@ -80,6 +76,7 @@
     def recv(dst, ss, rs, dev):
         pltpu.make_async_remote_copy(src_ref=dst, dst_ref=dst, send_sem=ss, recv_sem=rs, device_id=dev, device_id_type=MESH).wait_recv()
 
+    x_order = sorted(range(1, nx), key=lambda d: -min(d, nx - d))
     y_order = [2, 1, 3] if ny == 4 else list(range(1, ny))
     chunk_k = 128
     chunk = chunk_k * heads
@@ -104,12 +101,14 @@
         ssq = jnp.sum(sq, axis=1, keepdims=True)
         row = jnp.sum(jnp.where(diag, ssq, 0.0), axis=0, keepdims=True)
         ss_rx[n, my] = jnp.broadcast_to(row, (8, 128))
+        inv = lax.rsqrt(ssq / d_loc + EPS)
+        for j in range(nx):
+            h_v[:, j * cb:(j + 1) * cb] = (blocks[j] * inv * gain[:, j * cb:(j + 1) * cb].astype(F32)).astype(BF16)
+
+    def send_sums(n):
         for d in y_order:
             peer = lax.rem(my + d, ny)
             send(ss_rx.at[n, my], ss_rx.at[n, my], ss_ss.at[n, peer], ss_rs.at[n, my], {"y": peer})
-        inv = lax.rsqrt(ssq / d_loc + EPS)
-        for j in range(nx):
-            h_v[:, j * cb:(j + 1) * cb] = (blocks[j] * inv * gain[:, j * cb:(j + 1) * cb].astype(F32)).astype(BF16)
 
     def ratio_rows(n):
         for d in y_order:
@@ -126,25 +125,21 @@
     def to_column(row, index):
         return jnp.sum(jnp.where(lax.broadcasted_iota(jnp.int32, index.shape, 1) == index, row, 0.0), axis=1, keepdims=True)
 
-    def x_reduce(p, matmul):
-        for dc in ([2, 1, 3, 0] if chips == 4 else list(range(1, chips)) + [0]):
-            chip = lax.rem(my_chip + dc, chips)
-            part = matmul(pl.multiple_of(chip * 2 * cb, 2 * cb)).astype(BF16)
-            rs_tx[p, 2 * chip] = part[:, :cb]
-            rs_tx[p, 2 * chip + 1] = part[:, cb:]
-            if dc:
-                for core in range(2):
-                    dst = 2 * chip + core
-                    send(rs_tx.at[p, dst], rs_rx.at[p, mx], rs_ss.at[p, dst], rs_rs.at[p, mx], {"x": dst})
-            else:
-                send(rs_tx.at[p, partner], rs_rx.at[p, mx], rs_ss.at[p, partner], rs_rs.at[p, mx], {"x": partner})
-        total = rs_tx[p, mx].astype(F32)
-        for d in [nx - d for d in range(1, nx)]:
+    def x_reduce(p, part, fill=None):
+        for j in range(nx):
+            rs_tx[p, j] = part[:, j * cb:(j + 1) * cb].astype(BF16)
+        for d in x_order:
+            dst = lax.rem(mx + d, nx)
+            send(rs_tx.at[p, dst], rs_rx.at[p, mx], rs_ss.at[p, dst], rs_rs.at[p, mx], {"x": dst})
+        if fill is not None:
+            fill()
+        total = xg[p, mx].astype(F32) + rs_tx[p, mx].astype(F32)
+        for d in reversed(x_order):
             src = lax.rem(mx + d, nx)
             recv(rs_rx.at[p, src], rs_ss.at[p, src], rs_rs.at[p, src], {"x": src})
             total = total + rs_rx[p, src].astype(F32)
-        xg[p + 1, mx] = (xg[p, mx].astype(F32) + total).astype(BF16)
-        for d in [4, 3, 5, 2, 6, 1, 7]:
+        xg[p + 1, mx] = total.astype(BF16)
+        for d in x_order:
             dst = lax.rem(mx + d, nx)
             send(xg.at[p + 1, mx], xg.at[p + 1, mx], ag_ss.at[p, dst], ag_rs.at[p, mx], {"x": dst})
 
@@ -156,18 +151,6 @@
     loads["hid"].wait()
     for j in range(nx):
         xg[0, j] = hid_v[:, j * cb:(j + 1) * cb]
-    for j in range(3):
-        loads["w", 0, j].wait()
-        relayout(0, j)
-    loads["na"].wait()
-    loads["len"].wait()
-    loads["rel"].wait()
-    loads["bu"].wait()
-    loads["bw"].wait()
-    loads["nm"].wait()
-    pl.semaphore_wait(barrier, ny - 1 + nx - 1)
-
-    cell_row = lax.broadcasted_iota(jnp.int32, (cells, 1), 0)
     key_lane = lax.broadcasted_iota(jnp.int32, (cells, kl), 1)
     key_row = lax.broadcasted_iota(jnp.int32, (cells, kl), 0)
     group_row = lax.broadcasted_iota(jnp.int32, (16, 1), 0) // heads
@@ -182,10 +165,47 @@
         for h in range(heads):
             r0_v[l, pl.ds(h, rb, stride=heads), :] = jnp.broadcast_to(first[h:h + 1], (rb, hd))
 
+    def merge(l, new, tile_s, cache):
+        for i in range(per_group):
+            for h in range(heads):
+                tile_s[pl.ds(i * heads + h, rb, stride=16), :] = new[:, h * hd:(h + 1) * hd]
+        for b in range(rb):
+            tile = tile_s[16 * b:16 * b + 16].astype(BF16)
+            at = lent_s[16 * b:16 * b + 16].astype(BF16)
+            full = jnp.broadcast_to(tile[None], (kl // 16, 16, hd)).reshape(kl, hd)
+            where_at = jnp.broadcast_to(at[None], (kl // 16, 16, hd)).reshape(kl, hd)
+            cache[l, b] = jnp.where(pos_v[...] == where_at, full, cache[l, b])
+
+    def prepare_lengths():
+        pos_v[...] = (lax.broadcasted_iota(jnp.int32, (kl, hd), 0) // heads).astype(F32).astype(BF16)
+        index = my * rb + lax.broadcasted_iota(jnp.int32, (16 * rb, rows), 0) // 16
+        lent_s[...] = jnp.broadcast_to(to_column(len_v[...].astype(F32), index), (16 * rb, hd))
+
+    def early_relayout(l, j):
+        loads["w", l, j].wait()
+        relayout(l, j)
+
+    fills = {}
+    if layers > 1:
+        fills = {"q": lambda l: early_relayout(l, 0), "up": lambda l: early_relayout(l, 1), "rs": lambda l: early_relayout(l, 2), "rs2": prepare_rel}
+
+    def fill_for(name, l):
+        return None if l >= layers or name not in fills else (lambda: fills[name](l))
+
     for l in range(layers):
         p = 2 * l
-        norm_stage(2 * l, p, na_v[l:l + 1])
+        if l == 0:
+            loads["na"].wait()
+        norm_stage(p, p, na_v[l:l + 1])
+        if l:
+            send_sums(p)
         for j in range(3):
+            if l == 0:
+                loads["w", 0, j].wait()
+                relayout(0, j)
+                if j == 0:
+                    pl.semaphore_wait(barrier, ny - 1 + nx - 1)
+                    send_sums(p)
             part = jnp.dot(h_v[...], wqkv_v[l, :, j * hh:(j + 1) * hh], preferred_element_type=F32)
             qkv_tx[l, j] = part.astype(BF16)
             for d in y_order:
@@ -196,12 +216,14 @@
         for j in range(3):
             qkv_rx[l, my, j] = qkv_tx[l, j, pl.ds(own_at, rb), :]
         if l == 0:
-            for l2 in range(layers):
-                prepare_rel(l2)
-            for l2 in range(1, layers):
-                for j in range(3):
-                    loads["w", l2, j].wait()
-                    relayout(l2, j)
+            for name in ("len", "rel", "bu", "bw", "nm"):
+                loads[name].wait()
+            prepare_lengths()
+            prepare_rel(0)
+            if "q" in fills:
+                fills["q"](1)
+        loads["k", l].wait()
+        loads["v", l].wait()
         lens_row = len_v[...].astype(F32)
         want = my * rb + lax.broadcasted_iota(jnp.int32, (cells, rows), 0) // heads
         lens = to_column(lens_row, want).astype(jnp.int32)
@@ -232,7 +254,6 @@
             rolled = pltpu.roll(rel, kl - bit * heads, 1)
             rel = jnp.where(lax.rem(shift // bit, 2) == 1, rolled, rel)
             bit *= 2
-        loads["k", l].wait()
         score_parts = []
         for g in range(cells // 16):
             ag = a[16 * g:16 * g + 16]
@@ -249,8 +270,6 @@
             v_s[pl.ds(h, rb, stride=heads), :] = v[:, h * hd:(h + 1) * hd]
         kn = k_s[...]
         vn = v_s[...]
-        kn_v[l] = kn.astype(BF16)
-        vn_v[l] = vn.astype(BF16)
         scale = hd ** -0.5
         s_new = (jnp.sum(a.astype(F32) * kn, axis=1, keepdims=True) + jnp.sum(c.astype(F32) * r0_v[l], axis=1, keepdims=True)) * scale
         valid = (lax.rem(key_lane, heads) == lax.rem(key_row, heads)) & (key_lane // heads < lens)
@@ -261,7 +280,6 @@
         inv_den = 1.0 / (jnp.sum(e, axis=1, keepdims=True) + e_new)
         prob = (e * inv_den).astype(BF16)
         p_new = (e_new * inv_den).astype(BF16).astype(F32)
-        loads["v", l].wait()
         ctx_parts = []
         for g in range(cells // 16):
             pg = prob[16 * g:16 * g + 16]
@@ -279,15 +297,18 @@
         for d in y_order:
             peer = lax.rem(my + d, ny)
             send(ctx_all.at[l, my], ctx_all.at[l, my], ctx_ss.at[l, peer], ctx_rs.at[l, my], {"y": peer})
+        merge(l, k, kt_s, kc_v)
+        merge(l, v, vt_s, vc_v)
         loads["o", l].wait()
-        for d in y_order:
+        for d in reversed(y_order):
             src = lax.rem(my + d, ny)
             recv(ctx_all.at[l, src], ctx_ss.at[l, src], ctx_rs.at[l, src], {"y": src})
         ctx = jnp.concatenate([ctx_all[l, s] for s in range(ny)], axis=0)
-        x_reduce(p, lambda at: jnp.dot(ctx, wo_v[l, :, pl.ds(at, 2 * cb)], preferred_element_type=F32))
+        x_reduce(p, jnp.dot(ctx, wo_v[l], preferred_element_type=F32), fill_for("rs", l + 1))
         x_gather_wait(p)
         p = 2 * l + 1
         norm_stage(p, p, nm_v[l:l + 1])
+        send_sums(p)
         loads["up", l].wait()
         for d in y_order + [0]:
             dst = lax.rem(my + d, ny)
@@ -297,6 +318,8 @@
                 send(up_tx.at[l, dst], up_rx.at[l, my], up_ss.at[l, dst], up_rs.at[l, my], {"y": dst})
             else:
                 up_rx[l, my] = part
+        if fill_for("up", l + 1) is not None:
+            fills["up"](l + 1)
         ratios = ratio_rows(p)
         cols = [to_column(r, rown) for r in ratios]
         for d in y_order:
@@ -321,53 +344,28 @@
             acc_v[...] += jnp.dot(act[l, src], wdn_v[l, down_rows(src), :], preferred_element_type=F32)
         src = lax.rem(my + y_order[0], ny)
         recv(act.at[l, src], act_ss.at[l, src], act_rs.at[l, src], {"y": src})
-        x_reduce(p, lambda at: acc_v[:, pl.ds(at, 2 * cb)] + jnp.dot(act[l, src], wdn_v[l, down_rows(src), pl.ds(at, 2 * cb)], preferred_element_type=F32))
+        x_reduce(p, acc_v[...] + jnp.dot(act[l, src], wdn_v[l, down_rows(src), :], preferred_element_type=F32), fill_for("rs2", l + 1))
         x_gather_wait(p)
 
     last = 2 * layers
     for j in range(nx):
-        outh_v[:, j * cb:(j + 1) * cb] = xg[last, j]
-    outs = [pltpu.make_async_copy(outh_v, hid_out, out_sem.at[0]),
-            pltpu.make_async_copy(kn_v, kn_out, out_sem.at[1]),
-            pltpu.make_async_copy(vn_v, vn_out, out_sem.at[2])]
-    for o in outs:
-        o.start()
+        hid_out[:, j * cb:(j + 1) * cb] = xg[last, j]
     for c in sends:
         c.wait_send()
-    for o in outs:
-        o.wait()
-
-
-def cache_kernel(dims, len_ref, hid_in, kc_in, vc_in, kn_in, vn_in, hid_out, kc_out, vc_out, hid_v, kc_v, vc_v, kn_v, vn_v, in_sem, out_sem):
-    layers, rb = dims
-    my = lax.axis_index("y")
-    ins = []
-    for i, (src, dst) in enumerate(((kn_in, kn_v), (vn_in, vn_v), (hid_in, hid_v))):
-        c = pltpu.make_async_copy(src, dst, in_sem.at[i])
+
+
+def write_kernel(hid_in, kc_in, vc_in, hid_out, kc_out, vc_out, sem):
+    copies = [pltpu.make_async_copy(hid_in, hid_out, sem.at[0])]
+    layers, rb = kc_in.shape[:2]
+    half = rb // 2
+    for src, dst in ((kc_in, kc_out), (vc_in, vc_out)):
+        for l in range(layers):
+            for b in range(0, rb, half):
+                copies.append(pltpu.make_async_copy(src.at[l, pl.ds(b, half)], dst.at[l, pl.ds(b, half)], sem.at[len(copies)]))
+    for c in copies:
         c.start()
-        ins.append(c)
-    half = rb // 2
-    parts = []
-    for l in range(layers):
-        for src, buf, new, dst in ((kc_in, kc_v, kn_v, kc_out), (vc_in, vc_v, vn_v, vc_out)):
-            for s in range(2):
-                at = pl.ds(s * half, half)
-                i = len(parts)
-                r = pltpu.make_async_copy(src.at[l, at], buf.at[l, at], in_sem.at[3 + i])
-                r.start()
-                parts.append((r, pltpu.make_async_copy(buf.at[l, at], dst.at[l, at], out_sem.at[1 + i]), buf, new, l, s * half))
-    for c in ins:
+    for c in copies:
         c.wait()
-    out_h = pltpu.make_async_copy(hid_v, hid_out, out_sem.at[0])
-    out_h.start()
-    for r, w, buf, new, l, b0 in parts:
-        r.wait()
-        for b in range(b0, b0 + half):
-            buf[l, b, len_ref[my * rb + b]] = new[l, b]
-        w.start()
-    out_h.wait()
-    for part in parts:
-        part[1].wait()
 
 
 def solution(mesh):
@@ -397,49 +395,47 @@
         dma = pltpu.SemaphoreType.DMA
         scratch = [
             vmem((rows, d_loc), BF16), vmem((1, rows), jnp.int32),
-            vmem((layers, rb, kl, hd), BF16), vmem((layers, rb, kl, hd), BF16),
             vmem((layers, kl, hd), BF16), vmem((layers, d_loc), BF16), vmem((layers, d_loc), BF16),
             vmem((layers, heads, hd), BF16), vmem((layers, heads, hd), BF16),
             vmem((layers, 3, d_loc * heads, hd), BF16), vmem((layers, d_loc, 3 * hh), BF16),
             vmem((layers, hh, d_loc), BF16), vmem((layers, d_loc, ff_loc), BF16), vmem((layers, ff_loc, d_loc), BF16),
             vmem((128 * heads, hd), F32), vmem((layers, kl, hd), BF16), vmem((layers, cells, hd), F32), vmem((rows, d_loc), BF16),
             vmem((cells, hd), F32), vmem((cells, hd), F32), vmem((cells, hd), F32), vmem((cells, hd), F32), vmem((cells, hd), F32),
-            vmem((layers, cells, hd), BF16), vmem((layers, cells, hd), BF16), vmem((rows, d_loc), F32), vmem((rows, d_loc), BF16),
+            vmem((rows, d_loc), F32), vmem((kl, hd), BF16), vmem((16 * rb, hd), F32), vmem((16 * rb, hd), F32), vmem((16 * rb, hd), F32),
             vmem((2 * layers, ny, 8, 128), F32),
             vmem((layers, 3, rows, hh), BF16), vmem((layers, ny, 3, rb, hh), BF16), vmem((layers, ny, rb, hh), BF16),
             vmem((2 * layers, nx, rows, cb), BF16), vmem((2 * layers, nx, rows, cb), BF16), vmem((2 * layers + 1, nx, rows, cb), BF16),
             vmem((layers, ny, rows, fb), BF16), vmem((layers, ny, rows, fb), BF16), vmem((layers, ny, rows, fb), BF16),
-            dma((7 + 8 * layers,)), dma((3,)),
+            dma((7 + 8 * layers,)),
             dma((2 * layers, ny)), dma((2 * layers, ny)), dma((layers, 3, ny)), dma((layers, 3, ny)),
             dma((layers, ny)), dma((layers, ny)), dma((2 * layers, nx)), dma((2 * layers, nx)),
             dma((2 * layers, nx)), dma((2 * layers, nx)), dma((layers, ny)), dma((layers, ny)), dma((layers, ny)), dma((layers, ny)),
         ]
-        new_shape = jax.ShapeDtypeStruct((layers, cells, hd), BF16)
+        cache_dims = (layers, rb, kl, hd)
+        vmem_spec = pl.BlockSpec(memory_space=vmem)
         hid, k_new, v_new = pl.pallas_call(
             functools.partial(step_kernel, dims),
-            out_shape=(jax.ShapeDtypeStruct((rows, d_loc), BF16), new_shape, new_shape),
+            out_shape=(vmem((rows, d_loc), BF16), vmem(cache_dims, BF16), vmem(cache_dims, BF16)),
             in_specs=[any_spec] * 15,
-            out_specs=(any_spec,) * 3,
+            out_specs=(vmem_spec,) * 3,
             scratch_shapes=scratch,
-            compiler_params=pltpu.CompilerParams(collective_id=0, has_side_effects=True, vmem_limit_bytes=67043328),
+            compiler_params=pltpu.CompilerParams(collective_id=0, has_side_effects=True, vmem_limit_bytes=46 * 1024 * 1024),
             name="decode_step",
         )(hidden, lengths.reshape(1, rows), k_cache.reshape(layers, rb, kl, hd), v_cache.reshape(layers, rb, kl, hd),
           rel_table.reshape(layers, kl, hd), norm_attn,
           w_q.reshape(layers, d_loc * heads, hd), w_k.reshape(layers, d_loc * heads, hd), w_v.reshape(layers, d_loc * heads, hd),
           bias_content, bias_pos, w_out.reshape(layers, hh, d_loc), norm_mlp, w_up, w_down)
 
-        cache_shape = jax.ShapeDtypeStruct(k_cache.shape, BF16)
-        return pl.pallas_call(
-            functools.partial(cache_kernel, (layers, rb)),
-            out_shape=(jax.ShapeDtypeStruct((rows, d_loc), BF16), cache_shape, cache_shape),
-            in_specs=[pl.BlockSpec(memory_space=pltpu.SMEM)] + [any_spec] * 5,
+        flat = jax.ShapeDtypeStruct(cache_dims, BF16)
+        hid, k_new, v_new = pl.pallas_call(
+            write_kernel,
+            out_shape=(jax.ShapeDtypeStruct((rows, d_loc), BF16), flat, flat),
+            in_specs=[vmem_spec] * 3,
             out_specs=(any_spec,) * 3,
-            scratch_shapes=[
-                vmem((rows, d_loc), BF16), vmem(k_cache.shape, BF16), vmem(k_cache.shape, BF16),
-                vmem((layers, rb, heads, hd), BF16), vmem((layers, rb, heads, hd), BF16),
-                dma((3 + 4 * layers,)), dma((1 + 4 * layers,)),
-            ],
+            scratch_shapes=[dma((1 + 4 * layers,))],
+            compiler_params=pltpu.CompilerParams(vmem_limit_bytes=2 * 1024 * 1024),
             name="cache_write",
-        )(lengths, hid, k_cache, v_cache, k_new.reshape(layers, rb, heads, hd), v_new.reshape(layers, rb, heads, hd))
+        )(hid, k_new, v_new)
+        return hid, k_new.reshape(k_cache.shape), v_new.reshape(v_cache.shape)
 
     return jax.shard_map(local_step, mesh=mesh, in_specs=in_specs, out_specs=out_specs, check_vma=False)

time: 93.2 us -> 87.2 us (0.936)
  Pallas kernels: 92.5 us -> 86.5 us
    pallas_call x2, Pallas kernels: 92.5 us -> 86.5 us  [the longest x1 83.1 us: local_step(): pl.pallas_call(functools.partial(step_kernel, dims), out_shape=(vmem((row...]
where the time goes in v2:
time: 87.2 us; the launch traced here: 87.1 us
  Pallas kernels  86.5 us (99%)
    pallas_call x1, Pallas kernels, local_step(): pl.pallas_call(functools.partial(step_kernel, dims), out_shape=(vmem((row...  83.1 us
    pallas_call x1, Pallas kernels, local_step(): pl.pallas_call(write_kernel, out_shape=(jax.ShapeDtypeStruct((rows, d_loc...  3.42 us

profile of v2, /device:TPU:97, one launch (start us, length us, event | category | flops | bytes accessed | tf_op | source)
XLA Modules:
  0.0 87.1 jit_solution(675969115661183909)
XLA Ops:
  0.6 83.1 %decode_step.1 = (bf16[64,1024]{1,0:T(8,128)(2,1)S(1)}, bf16[2,16,512,128]{3,2,1,0:T(8,128)(2,1)S(1)}, bf16[2,16,512,128]{3,2,1,0:T(8,128)(2,1)S(1)}) custom-call(bf16[64,1024]{1,0:T(8,128)(2,1)} %hidden_in.1, s32[1,64]{1,0:T(1,128)} %bitcast.17, bf16[2,16,512,128]{3,2,1,0:T(8,128)(2,1)} %bitcast.10, bf16[2,16,512,128]{3,2,1,0:T(8,128)(2,1)} %bitcast.11, ...), custom_call_target="tpu_custom_call" | custom-call | tf_op jit(solution)/shard_map/decode_step/pallas_call | solution.py:416
  83.7 3.4 %cache_write.1 = (bf16[64,1024]{1,0:T(8,128)(2,1)}, bf16[2,16,512,128]{3,2,1,0:T(8,128)(2,1)}, bf16[2,16,512,128]{3,2,1,0:T(8,128)(2,1)}) custom-call(bf16[64,1024]{1,0:T(8,128)(2,1)S(1)} %get-tuple-element.9.hid_in, bf16[2,16,512,128]{3,2,1,0:T(8,128)(2,1)S(1)} %get-tuple-element.10.kc_in, bf16[2,16,512,128]{3,2,1,0:T(8,128)(2,1)S(1)} %get-tuple-element.11.vc_in), custom_call_target="tpu_custom_call" | custom-call | tf_op jit(solution)/shard_map/cache_write/pallas_call | solution.py:430

commit v3 on v2

--- a/solution.py
+++ b/solution.py
@@ -16,7 +16,7 @@
 def step_kernel(dims, hidden_in, len_in, kc_in, vc_in, rel_in, na_in, wq_in, wk_in, wv_in, bu_in, bw_in, wo_in, nm_in, wup_in, wdn_in,
                 hid_out, kc_v, vc_v,
                 hid_v, len_v, rel_v, na_v, nm_v, bu_v, bw_v, wraw_v, wqkv_v, wo_v, wup_v, wdn_v,
-                wtmp, relf_v, r0_v, h_v, a_s, c_s, k_s, v_s, ctx_s, acc_v, pos_v, lent_s, kt_s, vt_s,
+                wtmp, relf_v, r0_v, h_v, a_s, c_s, k_s, v_s, ctx_s, acc_v, pos_v, lent_s, kt_s, vt_s, dg_v,
                 ss_rx, qkv_tx, qkv_rx, ctx_all, rs_tx, rs_rx, xg, up_tx, up_rx, act,
                 ld_sem, ss_ss, ss_rs, qkv_ss, qkv_rs, ctx_ss, ctx_rs, rs_ss, rs_rs, ag_ss, ag_rs, up_ss, up_rs, act_ss, act_rs):
     layers, ny, nx, rows, heads, hd, seq, d_loc, ff_loc = dims
@@ -27,8 +27,13 @@
     fb = ff_loc // ny
     cells = rb * heads
     kl = seq * heads
+    chips = nx // 2
+    pair = 2 * cb
+    fh = fb // 2
     my = lax.axis_index("y")
     mx = lax.axis_index("x")
+    my_chip = mx // 2
+    partner = mx + 1 - 2 * lax.rem(mx, 2)
 
     barrier = pltpu.get_barrier_semaphore()
     for d in range(1, ny):
@@ -93,14 +98,17 @@
     rown = lax.broadcasted_iota(jnp.int32, (rows, 128), 0)
     diag = lane == rown
 
+    def store_sums(n, ssq):
+        row = jnp.sum(jnp.where(diag, ssq, 0.0), axis=0, keepdims=True)
+        ss_rx[n, my] = jnp.broadcast_to(row, (8, 128))
+
     def norm_stage(n, p, gain):
         blocks = [xg[p, j].astype(F32) for j in range(nx)]
         sq = blocks[0] * blocks[0]
         for j in range(1, nx):
             sq = sq + blocks[j] * blocks[j]
         ssq = jnp.sum(sq, axis=1, keepdims=True)
-        row = jnp.sum(jnp.where(diag, ssq, 0.0), axis=0, keepdims=True)
-        ss_rx[n, my] = jnp.broadcast_to(row, (8, 128))
+        store_sums(n, ssq)
         inv = lax.rsqrt(ssq / d_loc + EPS)
         for j in range(nx):
             h_v[:, j * cb:(j + 1) * cb] = (blocks[j] * inv * gain[:, j * cb:(j + 1) * cb].astype(F32)).astype(BF16)
@@ -143,10 +151,43 @@
             dst = lax.rem(mx + d, nx)
             send(xg.at[p + 1, mx], xg.at[p + 1, mx], ag_ss.at[p, dst], ag_rs.at[p, mx], {"x": dst})
 
-    def x_gather_wait(p):
-        for d in range(1, nx):
-            src = lax.rem(mx + d, nx)
-            recv(xg.at[p + 1, src], ag_ss.at[p, src], ag_rs.at[p, src], {"x": src})
+    def recv_block(p, src):
+        recv(xg.at[p + 1, src], ag_ss.at[p, src], ag_rs.at[p, src], {"x": src})
+
+    groups = [[0]] + [sorted({d, chips - d}) for d in range(1, chips // 2 + 1)]
+
+    def scaled(p, gain, l, group):
+        at = [lax.rem(my_chip + dc, chips) for dc in group]
+        for dc, chip in zip(group, at):
+            if dc == 0:
+                recv_block(p, partner)
+            else:
+                recv_block(p, 2 * chip)
+                recv_block(p, 2 * chip + 1)
+        blocks = [jnp.concatenate([xg[p + 1, 2 * chip], xg[p + 1, 2 * chip + 1]], axis=1).astype(F32) for chip in at]
+        ssq = jnp.sum(sum(b * b for b in blocks), axis=1, keepdims=True)
+        inv = lax.rsqrt(ssq / (pair * len(group)) + EPS)
+        spans = [pl.ds(pl.multiple_of(chip * pair, pair), pair) for chip in at]
+        return ssq, [((b * inv * gain[l:l + 1, sp].astype(F32)).astype(BF16), sp) for b, sp in zip(blocks, spans)]
+
+    def gather_matmul(n, p, gain, l, weight, columns):
+        sums = []
+        for i, group in enumerate(groups):
+            ssq, hs = scaled(p, gain, l, group)
+            sums.append(ssq)
+            if i + 1 < len(groups):
+                for c in range(0, columns, 512):
+                    dg_v[i, :, c:c + 512] = sum(jnp.dot(h, weight[l, sp, c:c + 512], preferred_element_type=F32) for h, sp in hs)
+        total = sum(sums)
+        store_sums(n, total)
+        send_sums(n)
+        inv = lax.rsqrt(total / d_loc + EPS)
+        factors = [jnp.where(total < jnp.inf, inv * jnp.sqrt(q / (pair * len(g)) + EPS), 0.0) for q, g in zip(sums, groups)]
+
+        def product(c, width):
+            last = sum(jnp.dot(h, weight[l, sp, c:c + width], preferred_element_type=F32) for h, sp in hs)
+            return sum(f * dg_v[i, :, c:c + width] for i, f in enumerate(factors[:-1])) + factors[-1] * last
+        return product
 
     loads["hid"].wait()
     for j in range(nx):
@@ -194,34 +235,36 @@
 
     for l in range(layers):
         p = 2 * l
-        if l == 0:
-            loads["na"].wait()
-        norm_stage(p, p, na_v[l:l + 1])
-        if l:
-            send_sums(p)
-        for j in range(3):
-            if l == 0:
-                loads["w", 0, j].wait()
-                relayout(0, j)
-                if j == 0:
-                    pl.semaphore_wait(barrier, ny - 1 + nx - 1)
-                    send_sums(p)
-            part = jnp.dot(h_v[...], wqkv_v[l, :, j * hh:(j + 1) * hh], preferred_element_type=F32)
-            qkv_tx[l, j] = part.astype(BF16)
+        def send_qkv(j):
             for d in y_order:
                 peer = lax.rem(my + d, ny)
                 rows_at = pl.multiple_of(peer * rb, rb)
                 send(qkv_tx.at[l, j, pl.ds(rows_at, rb)], qkv_rx.at[l, my, j], qkv_ss.at[l, j, peer], qkv_rs.at[l, j, my], {"y": peer})
+
+        if l == 0:
+            loads["na"].wait()
+            norm_stage(p, p, na_v[l:l + 1])
+            for j in range(3):
+                early_relayout(0, j)
+                qkv_tx[l, j] = jnp.dot(h_v[...], wqkv_v[l, :, j * hh:(j + 1) * hh], preferred_element_type=F32).astype(BF16)
+                if j == 1:
+                    pl.semaphore_wait(barrier, ny - 1 + nx - 1)
+                    send_sums(p)
+                    send_qkv(0)
+                if j:
+                    send_qkv(j)
+        else:
+            product = gather_matmul(p, p - 1, na_v, l, wqkv_v, 3 * hh)
+            for j in range(3):
+                qkv_tx[l, j] = product(j * hh, hh).astype(BF16)
+                send_qkv(j)
         own_at = pl.multiple_of(my * rb, rb)
         for j in range(3):
             qkv_rx[l, my, j] = qkv_tx[l, j, pl.ds(own_at, rb), :]
         if l == 0:
             for name in ("len", "rel", "bu", "bw", "nm"):
                 loads[name].wait()
-            prepare_lengths()
             prepare_rel(0)
-            if "q" in fills:
-                fills["q"](1)
         loads["k", l].wait()
         loads["v", l].wait()
         lens_row = len_v[...].astype(F32)
@@ -286,8 +329,8 @@
             cg = None
             for i in range(0, per_group, 2):
                 b = g * per_group + i
-                pair = jnp.concatenate([vc_v[l, b], vc_v[l, b + 1]], axis=1)
-                o = jnp.dot(pg, pair, preferred_element_type=F32)
+                values = jnp.concatenate([vc_v[l, b], vc_v[l, b + 1]], axis=1)
+                o = jnp.dot(pg, values, preferred_element_type=F32)
                 cg = o[:, :hd] if cg is None else jnp.where(group_row == i, o[:, :hd], cg)
                 cg = jnp.where(group_row == i + 1, o[:, hd:], cg)
             ctx_parts.append(cg)
@@ -297,6 +340,10 @@
         for d in y_order:
             peer = lax.rem(my + d, ny)
             send(ctx_all.at[l, my], ctx_all.at[l, my], ctx_ss.at[l, peer], ctx_rs.at[l, my], {"y": peer})
+        if l == 0:
+            prepare_lengths()
+        if fill_for("q", l + 1) is not None:
+            fills["q"](l + 1)
         merge(l, k, kt_s, kc_v)
         merge(l, v, vt_s, vc_v)
         loads["o", l].wait()
@@ -305,47 +352,47 @@
             recv(ctx_all.at[l, src], ctx_ss.at[l, src], ctx_rs.at[l, src], {"y": src})
         ctx = jnp.concatenate([ctx_all[l, s] for s in range(ny)], axis=0)
         x_reduce(p, jnp.dot(ctx, wo_v[l], preferred_element_type=F32), fill_for("rs", l + 1))
-        x_gather_wait(p)
         p = 2 * l + 1
-        norm_stage(p, p, nm_v[l:l + 1])
-        send_sums(p)
         loads["up", l].wait()
-        for d in y_order + [0]:
-            dst = lax.rem(my + d, ny)
-            part = jnp.dot(h_v[...], wup_v[l, :, pl.ds(pl.multiple_of(dst * fb, fb), fb)], preferred_element_type=F32).astype(BF16)
-            if d:
-                up_tx[l, dst] = part
-                send(up_tx.at[l, dst], up_rx.at[l, my], up_ss.at[l, dst], up_rs.at[l, my], {"y": dst})
-            else:
-                up_rx[l, my] = part
+        product = gather_matmul(p, p - 1, nm_v, l, wup_v, ff_loc)
+        for hf in range(2):
+            for j in range(ny):
+                up_tx[l, hf, j] = product(j * fb + hf * fh, fh).astype(BF16)
+            for d in y_order:
+                dst = lax.rem(my + d, ny)
+                send(up_tx.at[l, hf, dst], up_rx.at[l, hf, my], up_ss.at[l, hf, dst], up_rs.at[l, hf, my], {"y": dst})
+        for hf in range(2):
+            up_rx[l, hf, my] = up_tx[l, hf, my]
         if fill_for("up", l + 1) is not None:
             fills["up"](l + 1)
         ratios = ratio_rows(p)
         cols = [to_column(r, rown) for r in ratios]
-        for d in y_order:
+        loads["dn", l].wait()
+        for hf in range(2):
+            for d in reversed(y_order):
+                src = lax.rem(my + d, ny)
+                recv(up_rx.at[l, hf, src], up_ss.at[l, hf, src], up_rs.at[l, hf, src], {"y": src})
+            tot = up_rx[l, hf, 0].astype(F32) * cols[0]
+            for s in range(1, ny):
+                tot = tot + up_rx[l, hf, s].astype(F32) * cols[s]
+            act[l, hf, my] = jax.nn.gelu(tot.astype(BF16).astype(F32), approximate=True).astype(BF16)
+            for d in y_order:
+                peer = lax.rem(my + d, ny)
+                send(act.at[l, hf, my], act.at[l, hf, my], act_ss.at[l, hf, peer], act_rs.at[l, hf, my], {"y": peer})
+
+        def down(hf, src):
+            return jnp.dot(act[l, hf, src], wdn_v[l, pl.ds(pl.multiple_of(src * fb + hf * fh, fh), fh), :], preferred_element_type=F32)
+
+        acc_v[...] = down(0, my) + down(1, my)
+        pieces = [(hf, d) for hf in range(2) for d in reversed(y_order)]
+        for hf, d in pieces:
             src = lax.rem(my + d, ny)
-            recv(up_rx.at[l, src], up_ss.at[l, src], up_rs.at[l, src], {"y": src})
-        tot = up_rx[l, 0].astype(F32) * cols[0]
-        for s in range(1, ny):
-            tot = tot + up_rx[l, s].astype(F32) * cols[s]
-        act[l, my] = jax.nn.gelu(tot.astype(BF16).astype(F32), approximate=True).astype(BF16)
-        for d in y_order:
-            peer = lax.rem(my + d, ny)
-            send(act.at[l, my], act.at[l, my], act_ss.at[l, peer], act_rs.at[l, my], {"y": peer})
-        loads["dn", l].wait()
-
-        def down_rows(src):
-            return pl.ds(pl.multiple_of(src * fb, fb), fb)
-
-        acc_v[...] = jnp.dot(act[l, my], wdn_v[l, down_rows(my), :], preferred_element_type=F32)
-        for d in reversed(y_order[1:]):
-            src = lax.rem(my + d, ny)
-            recv(act.at[l, src], act_ss.at[l, src], act_rs.at[l, src], {"y": src})
-            acc_v[...] += jnp.dot(act[l, src], wdn_v[l, down_rows(src), :], preferred_element_type=F32)
-        src = lax.rem(my + y_order[0], ny)
-        recv(act.at[l, src], act_ss.at[l, src], act_rs.at[l, src], {"y": src})
-        x_reduce(p, acc_v[...] + jnp.dot(act[l, src], wdn_v[l, down_rows(src), :], preferred_element_type=F32), fill_for("rs2", l + 1))
-        x_gather_wait(p)
+            recv(act.at[l, hf, src], act_ss.at[l, hf, src], act_rs.at[l, hf, src], {"y": src})
+            if (hf, d) != pieces[-1]:
+                acc_v[...] += down(hf, src)
+        x_reduce(p, acc_v[...] + down(hf, src), fill_for("rs2", l + 1))
+    for d in range(1, nx):
+        recv_block(2 * layers - 1, lax.rem(mx + d, nx))
 
     last = 2 * layers
     for j in range(nx):
@@ -402,14 +449,15 @@
             vmem((128 * heads, hd), F32), vmem((layers, kl, hd), BF16), vmem((layers, cells, hd), F32), vmem((rows, d_loc), BF16),
             vmem((cells, hd), F32), vmem((cells, hd), F32), vmem((cells, hd), F32), vmem((cells, hd), F32), vmem((cells, hd), F32),
             vmem((rows, d_loc), F32), vmem((kl, hd), BF16), vmem((16 * rb, hd), F32), vmem((16 * rb, hd), F32), vmem((16 * rb, hd), F32),
+            vmem((nx // 4, rows, max(ff_loc, 3 * hh)), F32),
             vmem((2 * layers, ny, 8, 128), F32),
             vmem((layers, 3, rows, hh), BF16), vmem((layers, ny, 3, rb, hh), BF16), vmem((layers, ny, rb, hh), BF16),
             vmem((2 * layers, nx, rows, cb), BF16), vmem((2 * layers, nx, rows, cb), BF16), vmem((2 * layers + 1, nx, rows, cb), BF16),
-            vmem((layers, ny, rows, fb), BF16), vmem((layers, ny, rows, fb), BF16), vmem((layers, ny, rows, fb), BF16),
+            vmem((layers, 2, ny, rows, fb // 2), BF16), vmem((layers, 2, ny, rows, fb // 2), BF16), vmem((layers, 2, ny, rows, fb // 2), BF16),
             dma((7 + 8 * layers,)),
             dma((2 * layers, ny)), dma((2 * layers, ny)), dma((layers, 3, ny)), dma((layers, 3, ny)),
             dma((layers, ny)), dma((layers, ny)), dma((2 * layers, nx)), dma((2 * layers, nx)),
-            dma((2 * layers, nx)), dma((2 * layers, nx)), dma((layers, ny)), dma((layers, ny)), dma((layers, ny)), dma((layers, ny)),
+            dma((2 * layers, nx)), dma((2 * layers, nx)), dma((layers, 2, ny)), dma((layers, 2, ny)), dma((layers, 2, ny)), dma((layers, 2, ny)),
         ]
         cache_dims = (layers, rb, kl, hd)
         vmem_spec = pl.BlockSpec(memory_space=vmem)

time: 87.2 us -> 86.2 us (0.989)
  Pallas kernels: 86.5 us -> 85.3 us
    pallas_call x1, Pallas kernels: 83.1 us -> 81.9 us  [local_step(): pl.pallas_call(functools.partial(step_kernel, dims), out_shape=(vmem((row...]
where the time goes in v3:
time: 86.2 us; the launch traced here: 86.1 us
  Pallas kernels  85.3 us (99%)
    pallas_call x1, Pallas kernels, local_step(): pl.pallas_call(functools.partial(step_kernel, dims), out_shape=(vmem((row...  81.9 us
    pallas_call x1, Pallas kernels, local_step(): pl.pallas_call(write_kernel, out_shape=(jax.ShapeDtypeStruct((rows, d_loc...  3.42 us

profile of v3, /device:TPU:97, one launch (start us, length us, event | category | flops | bytes accessed | tf_op | source)
XLA Modules:
  0.0 86.1 jit_solution(7153241666972345689)
XLA Ops:
  0.6 81.9 %decode_step.1 = (bf16[64,1024]{1,0:T(8,128)(2,1)S(1)}, bf16[2,16,512,128]{3,2,1,0:T(8,128)(2,1)S(1)}, bf16[2,16,512,128]{3,2,1,0:T(8,128)(2,1)S(1)}) custom-call(bf16[64,1024]{1,0:T(8,128)(2,1)} %hidden_in.1, s32[1,64]{1,0:T(1,128)} %bitcast.17, bf16[2,16,512,128]{3,2,1,0:T(8,128)(2,1)} %bitcast.10, bf16[2,16,512,128]{3,2,1,0:T(8,128)(2,1)} %bitcast.11, ...), custom_call_target="tpu_custom_call" | custom-call | tf_op jit(solution)/shard_map/decode_step/pallas_call | solution.py:464
  82.6 3.4 %cache_write.1 = (bf16[64,1024]{1,0:T(8,128)(2,1)}, bf16[2,16,512,128]{3,2,1,0:T(8,128)(2,1)}, bf16[2,16,512,128]{3,2,1,0:T(8,128)(2,1)}) custom-call(bf16[64,1024]{1,0:T(8,128)(2,1)S(1)} %get-tuple-element.9.hid_in, bf16[2,16,512,128]{3,2,1,0:T(8,128)(2,1)S(1)} %get-tuple-element.10.kc_in, bf16[2,16,512,128]{3,2,1,0:T(8,128)(2,1)S(1)} %get-tuple-element.11.vc_in), custom_call_target="tpu_custom_call" | custom-call | tf_op jit(solution)/shard_map/cache_write/pallas_call | solution.py:478

commit v4 on v3

--- a/solution.py
+++ b/solution.py
@@ -17,29 +17,31 @@
                 hid_out, kc_v, vc_v,
                 hid_v, len_v, rel_v, na_v, nm_v, bu_v, bw_v, wraw_v, wqkv_v, wo_v, wup_v, wdn_v,
                 wtmp, relf_v, r0_v, h_v, a_s, c_s, k_s, v_s, ctx_s, acc_v, pos_v, lent_s, kt_s, vt_s, dg_v,
-                ss_rx, qkv_tx, qkv_rx, ctx_all, rs_tx, rs_rx, xg, up_tx, up_rx, act,
-                ld_sem, ss_ss, ss_rs, qkv_ss, qkv_rs, ctx_ss, ctx_rs, rs_ss, rs_rs, ag_ss, ag_rs, up_ss, up_rs, act_ss, act_rs):
+                ss_rx, qkv_tx, qkv_rx, ctx_all, dd_tx, dd_rx, bc, xh, up_tx, up_rx, act,
+                ld_sem, ss_ss, ss_rs, qkv_ss, qkv_rs, ctx_ss, ctx_rs, dd_ss, dd_rs, bc_ss, bc_rs, xe_ss, xe_rs, up_ss, up_rs, act_ss, act_rs):
     layers, ny, nx, rows, heads, hd, seq, d_loc, ff_loc = dims
     d_total = d_loc * ny
     rb = rows // ny
     hh = heads * hd
-    cb = d_loc // nx
+    half = d_loc // 2
     fb = ff_loc // ny
     cells = rb * heads
     kl = seq * heads
     chips = nx // 2
-    pair = 2 * cb
     fh = fb // 2
     my = lax.axis_index("y")
     mx = lax.axis_index("x")
     my_chip = mx // 2
-    partner = mx + 1 - 2 * lax.rem(mx, 2)
+    core = lax.rem(mx, 2)
+    other = 1 - core
+    partner = {"x": 2 * my_chip + other}
 
     barrier = pltpu.get_barrier_semaphore()
     for d in range(1, ny):
         pl.semaphore_signal(barrier, inc=1, device_id={"y": lax.rem(my + d, ny)}, device_id_type=MESH)
-    for d in range(1, nx):
-        pl.semaphore_signal(barrier, inc=1, device_id={"x": lax.rem(mx + d, nx)}, device_id_type=MESH)
+    pl.semaphore_signal(barrier, inc=1, device_id=partner, device_id_type=MESH)
+    for d in range(1, chips):
+        pl.semaphore_signal(barrier, inc=1, device_id={"x": 2 * lax.rem(my_chip + d, chips) + core}, device_id_type=MESH)
 
     loads = {}
 
@@ -81,7 +83,7 @@
     def recv(dst, ss, rs, dev):
         pltpu.make_async_remote_copy(src_ref=dst, dst_ref=dst, send_sem=ss, recv_sem=rs, device_id=dev, device_id_type=MESH).wait_recv()
 
-    x_order = sorted(range(1, nx), key=lambda d: -min(d, nx - d))
+    chip_order = sorted(range(1, chips), key=lambda d: -min(d, chips - d))
     y_order = [2, 1, 3] if ny == 4 else list(range(1, ny))
     chunk_k = 128
     chunk = chunk_k * heads
@@ -103,15 +105,12 @@
         ss_rx[n, my] = jnp.broadcast_to(row, (8, 128))
 
     def norm_stage(n, p, gain):
-        blocks = [xg[p, j].astype(F32) for j in range(nx)]
-        sq = blocks[0] * blocks[0]
-        for j in range(1, nx):
-            sq = sq + blocks[j] * blocks[j]
-        ssq = jnp.sum(sq, axis=1, keepdims=True)
+        blocks = [xh[p, j].astype(F32) for j in range(2)]
+        ssq = jnp.sum(sum(b * b for b in blocks), axis=1, keepdims=True)
         store_sums(n, ssq)
         inv = lax.rsqrt(ssq / d_loc + EPS)
-        for j in range(nx):
-            h_v[:, j * cb:(j + 1) * cb] = (blocks[j] * inv * gain[:, j * cb:(j + 1) * cb].astype(F32)).astype(BF16)
+        for j in range(2):
+            h_v[:, j * half:(j + 1) * half] = (blocks[j] * inv * gain[:, j * half:(j + 1) * half].astype(F32)).astype(BF16)
 
     def send_sums(n):
         for d in y_order:
@@ -133,46 +132,46 @@
     def to_column(row, index):
         return jnp.sum(jnp.where(lax.broadcasted_iota(jnp.int32, index.shape, 1) == index, row, 0.0), axis=1, keepdims=True)
 
+    def half_at(which):
+        return pl.ds(pl.multiple_of(which * half, half), half)
+
     def x_reduce(p, part, fill=None):
-        for j in range(nx):
-            rs_tx[p, j] = part[:, j * cb:(j + 1) * cb].astype(BF16)
-        for d in x_order:
-            dst = lax.rem(mx + d, nx)
-            send(rs_tx.at[p, dst], rs_rx.at[p, mx], rs_ss.at[p, dst], rs_rs.at[p, mx], {"x": dst})
+        dd_tx[p] = part(half_at(other)).astype(BF16)
+        send(dd_tx.at[p], dd_rx.at[p], dd_ss.at[p], dd_rs.at[p], partner)
+        own = part(half_at(core))
+        recv(dd_rx.at[p], dd_ss.at[p], dd_rs.at[p], partner)
+        bc[p, my_chip] = (own + dd_rx[p].astype(F32)).astype(BF16)
+        for d in chip_order:
+            chip = lax.rem(my_chip + d, chips)
+            send(bc.at[p, my_chip], bc.at[p, my_chip], bc_ss.at[p, chip], bc_rs.at[p, my_chip], {"x": 2 * chip + core})
         if fill is not None:
             fill()
-        total = xg[p, mx].astype(F32) + rs_tx[p, mx].astype(F32)
-        for d in reversed(x_order):
-            src = lax.rem(mx + d, nx)
-            recv(rs_rx.at[p, src], rs_ss.at[p, src], rs_rs.at[p, src], {"x": src})
-            total = total + rs_rx[p, src].astype(F32)
-        xg[p + 1, mx] = total.astype(BF16)
-        for d in x_order:
-            dst = lax.rem(mx + d, nx)
-            send(xg.at[p + 1, mx], xg.at[p + 1, mx], ag_ss.at[p, dst], ag_rs.at[p, mx], {"x": dst})
-
-    def recv_block(p, src):
-        recv(xg.at[p + 1, src], ag_ss.at[p, src], ag_rs.at[p, src], {"x": src})
-
-    groups = [[0]] + [sorted({d, chips - d}) for d in range(1, chips // 2 + 1)]
-
-    def scaled(p, gain, l, group):
-        at = [lax.rem(my_chip + dc, chips) for dc in group]
-        for dc, chip in zip(group, at):
-            if dc == 0:
-                recv_block(p, partner)
-            else:
-                recv_block(p, 2 * chip)
-                recv_block(p, 2 * chip + 1)
-        blocks = [jnp.concatenate([xg[p + 1, 2 * chip], xg[p + 1, 2 * chip + 1]], axis=1).astype(F32) for chip in at]
-        ssq = jnp.sum(sum(b * b for b in blocks), axis=1, keepdims=True)
-        inv = lax.rsqrt(ssq / (pair * len(group)) + EPS)
-        spans = [pl.ds(pl.multiple_of(chip * pair, pair), pair) for chip in at]
-        return ssq, [((b * inv * gain[l:l + 1, sp].astype(F32)).astype(BF16), sp) for b, sp in zip(blocks, spans)]
+        for d in reversed(chip_order):
+            chip = lax.rem(my_chip + d, chips)
+            recv(bc.at[p, chip], bc_ss.at[p, chip], bc_rs.at[p, chip], {"x": 2 * chip + core})
+        total = xh[p, core].astype(F32)
+        for chip in range(chips):
+            total = total + bc[p, chip].astype(F32)
+        xh[p + 1, core] = total.astype(BF16)
+        send(xh.at[p + 1, core], xh.at[p + 1, core], xe_ss.at[p], xe_rs.at[p], partner)
+
+    def recv_half(p):
+        recv(xh.at[p + 1, other], xe_ss.at[p], xe_rs.at[p], partner)
+
+    groups = [core, other]
+
+    def scaled(p, gain, l, which):
+        block = xh[p + 1, which].astype(F32)
+        ssq = jnp.sum(block * block, axis=1, keepdims=True)
+        inv = lax.rsqrt(ssq / half + EPS)
+        at = half_at(which)
+        return ssq, [((block * inv * gain[l:l + 1, at].astype(F32)).astype(BF16), at)]
 
     def gather_matmul(n, p, gain, l, weight, columns):
         sums = []
         for i, group in enumerate(groups):
+            if i:
+                recv_half(p)
             ssq, hs = scaled(p, gain, l, group)
             sums.append(ssq)
             if i + 1 < len(groups):
@@ -182,7 +181,7 @@
         store_sums(n, total)
         send_sums(n)
         inv = lax.rsqrt(total / d_loc + EPS)
-        factors = [jnp.where(total < jnp.inf, inv * jnp.sqrt(q / (pair * len(g)) + EPS), 0.0) for q, g in zip(sums, groups)]
+        factors = [jnp.where(total < jnp.inf, inv * jnp.sqrt(q / half + EPS), 0.0) for q in sums]
 
         def product(c, width):
             last = sum(jnp.dot(h, weight[l, sp, c:c + width], preferred_element_type=F32) for h, sp in hs)
@@ -190,8 +189,8 @@
         return product
 
     loads["hid"].wait()
-    for j in range(nx):
-        xg[0, j] = hid_v[:, j * cb:(j + 1) * cb]
+    for j in range(2):
+        xh[0, j] = hid_v[:, j * half:(j + 1) * half]
     key_lane = lax.broadcasted_iota(jnp.int32, (cells, kl), 1)
     key_row = lax.broadcasted_iota(jnp.int32, (cells, kl), 0)
     group_row = lax.broadcasted_iota(jnp.int32, (16, 1), 0) // heads
@@ -248,7 +247,7 @@
                 early_relayout(0, j)
                 qkv_tx[l, j] = jnp.dot(h_v[...], wqkv_v[l, :, j * hh:(j + 1) * hh], preferred_element_type=F32).astype(BF16)
                 if j == 1:
-                    pl.semaphore_wait(barrier, ny - 1 + nx - 1)
+                    pl.semaphore_wait(barrier, ny - 1 + chips)
                     send_sums(p)
                     send_qkv(0)
                 if j:
@@ -351,7 +350,7 @@
             src = lax.rem(my + d, ny)
             recv(ctx_all.at[l, src], ctx_ss.at[l, src], ctx_rs.at[l, src], {"y": src})
         ctx = jnp.concatenate([ctx_all[l, s] for s in range(ny)], axis=0)
-        x_reduce(p, jnp.dot(ctx, wo_v[l], preferred_element_type=F32), fill_for("rs", l + 1))
+        x_reduce(p, lambda at: jnp.dot(ctx, wo_v[l, :, at], preferred_element_type=F32), fill_for("rs", l + 1))
         p = 2 * l + 1
         loads["up", l].wait()
         product = gather_matmul(p, p - 1, nm_v, l, wup_v, ff_loc)
@@ -380,8 +379,8 @@
                 peer = lax.rem(my + d, ny)
                 send(act.at[l, hf, my], act.at[l, hf, my], act_ss.at[l, hf, peer], act_rs.at[l, hf, my], {"y": peer})
 
-        def down(hf, src):
-            return jnp.dot(act[l, hf, src], wdn_v[l, pl.ds(pl.multiple_of(src * fb + hf * fh, fh), fh), :], preferred_element_type=F32)
+        def down(hf, src, at=slice(None)):
+            return jnp.dot(act[l, hf, src], wdn_v[l, pl.ds(pl.multiple_of(src * fb + hf * fh, fh), fh), at], preferred_element_type=F32)
 
         acc_v[...] = down(0, my) + down(1, my)
         pieces = [(hf, d) for hf in range(2) for d in reversed(y_order)]
@@ -390,13 +389,12 @@
             recv(act.at[l, hf, src], act_ss.at[l, hf, src], act_rs.at[l, hf, src], {"y": src})
             if (hf, d) != pieces[-1]:
                 acc_v[...] += down(hf, src)
-        x_reduce(p, acc_v[...] + down(hf, src), fill_for("rs2", l + 1))
-    for d in range(1, nx):
-        recv_block(2 * layers - 1, lax.rem(mx + d, nx))
+        x_reduce(p, lambda at: acc_v[:, at] + down(hf, src, at), fill_for("rs2", l + 1))
+    recv_half(2 * layers - 1)
 
     last = 2 * layers
-    for j in range(nx):
-        hid_out[:, j * cb:(j + 1) * cb] = xg[last, j]
+    for j in range(2):
+        hid_out[:, j * half:(j + 1) * half] = xh[last, j]
     for c in sends:
         c.wait_send()
 
@@ -434,7 +432,7 @@
         hh = heads * hd
         cells = rb * heads
         kl = seq * heads
-        cb = d_loc // nx
+        half = d_loc // 2
         fb = ff_loc // ny
         dims = (layers, ny, nx, rows, heads, hd, seq, d_loc, ff_loc)
         any_spec = pl.BlockSpec(memory_space=pl.ANY)
@@ -449,15 +447,15 @@
             vmem((128 * heads, hd), F32), vmem((layers, kl, hd), BF16), vmem((layers, cells, hd), F32), vmem((rows, d_loc), BF16),
             vmem((cells, hd), F32), vmem((cells, hd), F32), vmem((cells, hd), F32), vmem((cells, hd), F32), vmem((cells, hd), F32),
             vmem((rows, d_loc), F32), vmem((kl, hd), BF16), vmem((16 * rb, hd), F32), vmem((16 * rb, hd), F32), vmem((16 * rb, hd), F32),
-            vmem((nx // 4, rows, max(ff_loc, 3 * hh)), F32),
+            vmem((1, rows, max(ff_loc, 3 * hh)), F32),
             vmem((2 * layers, ny, 8, 128), F32),
             vmem((layers, 3, rows, hh), BF16), vmem((layers, ny, 3, rb, hh), BF16), vmem((layers, ny, rb, hh), BF16),
-            vmem((2 * layers, nx, rows, cb), BF16), vmem((2 * layers, nx, rows, cb), BF16), vmem((2 * layers + 1, nx, rows, cb), BF16),
+            vmem((2 * layers, rows, half), BF16), vmem((2 * layers, rows, half), BF16), vmem((2 * layers, nx // 2, rows, half), BF16), vmem((2 * layers + 1, 2, rows, half), BF16),
             vmem((layers, 2, ny, rows, fb // 2), BF16), vmem((layers, 2, ny, rows, fb // 2), BF16), vmem((layers, 2, ny, rows, fb // 2), BF16),
             dma((7 + 8 * layers,)),
             dma((2 * layers, ny)), dma((2 * layers, ny)), dma((layers, 3, ny)), dma((layers, 3, ny)),
-            dma((layers, ny)), dma((layers, ny)), dma((2 * layers, nx)), dma((2 * layers, nx)),
-            dma((2 * layers, nx)), dma((2 * layers, nx)), dma((layers, 2, ny)), dma((layers, 2, ny)), dma((layers, 2, ny)), dma((layers, 2, ny)),
+            dma((layers, ny)), dma((layers, ny)), dma((2 * layers,)), dma((2 * layers,)), dma((2 * layers, nx // 2)), dma((2 * layers, nx // 2)),
+            dma((2 * layers,)), dma((2 * layers,)), dma((layers, 2, ny)), dma((layers, 2, ny)), dma((layers, 2, ny)), dma((layers, 2, ny)),
         ]
         cache_dims = (layers, rb, kl, hd)
         vmem_spec = pl.BlockSpec(memory_space=vmem)

time: 86.2 us -> 81.6 us (0.947)
  Pallas kernels: 85.3 us -> 80.9 us
    pallas_call x1, Pallas kernels: 81.9 us -> 77.5 us  [local_step(): pl.pallas_call(functools.partial(step_kernel, dims), out_shape=(vmem((row...]
where the time goes in v4:
time: 81.6 us
  Pallas kernels  80.9 us (99%)
    pallas_call x1, Pallas kernels, local_step(): pl.pallas_call(functools.partial(step_kernel, dims), out_shape=(vmem((row...  77.5 us
    pallas_call x1, Pallas kernels, local_step(): pl.pallas_call(write_kernel, out_shape=(jax.ShapeDtypeStruct((rows, d_loc...  3.42 us

profile of v4, /device:TPU:97, one launch (start us, length us, event | category | flops | bytes accessed | tf_op | source)
XLA Modules:
  0.0 81.6 jit_solution(7760211165140740947)
XLA Ops:
  0.6 77.5 %decode_step.1 = (bf16[64,1024]{1,0:T(8,128)(2,1)S(1)}, bf16[2,16,512,128]{3,2,1,0:T(8,128)(2,1)S(1)}, bf16[2,16,512,128]{3,2,1,0:T(8,128)(2,1)S(1)}) custom-call(bf16[64,1024]{1,0:T(8,128)(2,1)} %hidden_in.1, s32[1,64]{1,0:T(1,128)} %bitcast.17, bf16[2,16,512,128]{3,2,1,0:T(8,128)(2,1)} %bitcast.10, bf16[2,16,512,128]{3,2,1,0:T(8,128)(2,1)} %bitcast.11, ...), custom_call_target="tpu_custom_call" | custom-call | tf_op jit(solution)/shard_map/decode_step/pallas_call | solution.py:462
  78.1 3.4 %cache_write.1 = (bf16[64,1024]{1,0:T(8,128)(2,1)}, bf16[2,16,512,128]{3,2,1,0:T(8,128)(2,1)}, bf16[2,16,512,128]{3,2,1,0:T(8,128)(2,1)}) custom-call(bf16[64,1024]{1,0:T(8,128)(2,1)S(1)} %get-tuple-element.9.hid_in, bf16[2,16,512,128]{3,2,1,0:T(8,128)(2,1)S(1)} %get-tuple-element.10.kc_in, bf16[2,16,512,128]{3,2,1,0:T(8,128)(2,1)S(1)} %get-tuple-element.11.vc_in), custom_call_target="tpu_custom_call" | custom-call | tf_op jit(solution)/shard_map/cache_write/pallas_call | solution.py:476

commit v5 on v4

--- a/solution.py
+++ b/solution.py
@@ -28,7 +28,8 @@
     cells = rb * heads
     kl = seq * heads
     chips = nx // 2
-    fh = fb // 2
+    fw = fb // 2
+    fh = fw // 2
     my = lax.axis_index("y")
     mx = lax.axis_index("x")
     my_chip = mx // 2
@@ -84,7 +85,8 @@
         pltpu.make_async_remote_copy(src_ref=dst, dst_ref=dst, send_sem=ss, recv_sem=rs, device_id=dev, device_id_type=MESH).wait_recv()
 
     chip_order = sorted(range(1, chips), key=lambda d: -min(d, chips - d))
-    y_order = [2, 1, 3] if ny == 4 else list(range(1, ny))
+    y_order = list(range(1, ny))
+    down_order = sorted(y_order, key=lambda d: min(d, ny - d))
     chunk_k = 128
     chunk = chunk_k * heads
 
@@ -183,9 +185,9 @@
         inv = lax.rsqrt(total / d_loc + EPS)
         factors = [jnp.where(total < jnp.inf, inv * jnp.sqrt(q / half + EPS), 0.0) for q in sums]
 
-        def product(c, width):
-            last = sum(jnp.dot(h, weight[l, sp, c:c + width], preferred_element_type=F32) for h, sp in hs)
-            return sum(f * dg_v[i, :, c:c + width] for i, f in enumerate(factors[:-1])) + factors[-1] * last
+        def product(at):
+            last = sum(jnp.dot(h, weight[l, sp, at], preferred_element_type=F32) for h, sp in hs)
+            return sum(f * dg_v[i, :, at] for i, f in enumerate(factors[:-1])) + factors[-1] * last
         return product
 
     loads["hid"].wait()
@@ -255,7 +257,7 @@
         else:
             product = gather_matmul(p, p - 1, na_v, l, wqkv_v, 3 * hh)
             for j in range(3):
-                qkv_tx[l, j] = product(j * hh, hh).astype(BF16)
+                qkv_tx[l, j] = product(slice(j * hh, (j + 1) * hh)).astype(BF16)
                 send_qkv(j)
         own_at = pl.multiple_of(my * rb, rb)
         for j in range(3):
@@ -291,11 +293,15 @@
         c = c_s[...].astype(BF16)
         rel = lax.dot_general(c, relf_v[l], (((1,), (1,)), ((), ())), preferred_element_type=F32)
         shift = seq - 1 - lens
-        bit = 1
-        while bit < seq:
-            rolled = pltpu.roll(rel, kl - bit * heads, 1)
-            rel = jnp.where(lax.rem(shift // bit, 2) == 1, rolled, rel)
-            bit *= 2
+        unit = 1
+        while unit < seq:
+            digit = lax.rem(shift // unit, 4)
+            rolled = rel
+            for m in range(1, 4):
+                if m * unit < seq:
+                    rolled = jnp.where(digit == m, pltpu.roll(rel, kl - m * unit * heads, 1), rolled)
+            rel = rolled
+            unit *= 4
         score_parts = []
         for g in range(cells // 16):
             ag = a[16 * g:16 * g + 16]
@@ -354,20 +360,26 @@
         p = 2 * l + 1
         loads["up", l].wait()
         product = gather_matmul(p, p - 1, nm_v, l, wup_v, ff_loc)
-        for hf in range(2):
-            for j in range(ny):
-                up_tx[l, hf, j] = product(j * fb + hf * fh, fh).astype(BF16)
+        def up_blocks(w, dst, to):
+            block = product(pl.ds(pl.multiple_of(dst * fb + w * fw, fw), fw)).astype(BF16)
+            for i in range(2):
+                to[l, 2 * w + i, dst] = block[:, i * fh:(i + 1) * fh]
+
+        for w in range(2):
             for d in y_order:
-                dst = lax.rem(my + d, ny)
-                send(up_tx.at[l, hf, dst], up_rx.at[l, hf, my], up_ss.at[l, hf, dst], up_rs.at[l, hf, my], {"y": dst})
-        for hf in range(2):
-            up_rx[l, hf, my] = up_tx[l, hf, my]
+                up_blocks(w, lax.rem(my + d, ny), up_tx)
+            for hf in (2 * w, 2 * w + 1):
+                for d in y_order:
+                    dst = lax.rem(my + d, ny)
+                    send(up_tx.at[l, hf, dst], up_rx.at[l, hf, my], up_ss.at[l, hf, dst], up_rs.at[l, hf, my], {"y": dst})
+        for w in range(2):
+            up_blocks(w, my, up_rx)
         if fill_for("up", l + 1) is not None:
             fills["up"](l + 1)
         ratios = ratio_rows(p)
         cols = [to_column(r, rown) for r in ratios]
         loads["dn", l].wait()
-        for hf in range(2):
+        for hf in range(4):
             for d in reversed(y_order):
                 src = lax.rem(my + d, ny)
                 recv(up_rx.at[l, hf, src], up_ss.at[l, hf, src], up_rs.at[l, hf, src], {"y": src})
@@ -379,17 +391,19 @@
                 peer = lax.rem(my + d, ny)
                 send(act.at[l, hf, my], act.at[l, hf, my], act_ss.at[l, hf, peer], act_rs.at[l, hf, my], {"y": peer})
 
-        def down(hf, src, at=slice(None)):
-            return jnp.dot(act[l, hf, src], wdn_v[l, pl.ds(pl.multiple_of(src * fb + hf * fh, fh), fh), at], preferred_element_type=F32)
+        def down(w, src, at=slice(None)):
+            pieces = jnp.concatenate([act[l, 2 * w, src], act[l, 2 * w + 1, src]], axis=1)
+            return jnp.dot(pieces, wdn_v[l, pl.ds(pl.multiple_of(src * fb + w * fw, fw), fw), at], preferred_element_type=F32)
 
         acc_v[...] = down(0, my) + down(1, my)
-        pieces = [(hf, d) for hf in range(2) for d in reversed(y_order)]
-        for hf, d in pieces:
+        steps = [(w, d) for w in range(2) for d in down_order]
+        for w, d in steps:
             src = lax.rem(my + d, ny)
-            recv(act.at[l, hf, src], act_ss.at[l, hf, src], act_rs.at[l, hf, src], {"y": src})
-            if (hf, d) != pieces[-1]:
-                acc_v[...] += down(hf, src)
-        x_reduce(p, lambda at: acc_v[:, at] + down(hf, src, at), fill_for("rs2", l + 1))
+            for hf in (2 * w, 2 * w + 1):
+                recv(act.at[l, hf, src], act_ss.at[l, hf, src], act_rs.at[l, hf, src], {"y": src})
+            if (w, d) != steps[-1]:
+                acc_v[...] += down(w, src)
+        x_reduce(p, lambda at: acc_v[:, at] + down(w, src, at), fill_for("rs2", l + 1))
     recv_half(2 * layers - 1)
 
     last = 2 * layers
@@ -451,11 +465,11 @@
             vmem((2 * layers, ny, 8, 128), F32),
             vmem((layers, 3, rows, hh), BF16), vmem((layers, ny, 3, rb, hh), BF16), vmem((layers, ny, rb, hh), BF16),
             vmem((2 * layers, rows, half), BF16), vmem((2 * layers, rows, half), BF16), vmem((2 * layers, nx // 2, rows, half), BF16), vmem((2 * layers + 1, 2, rows, half), BF16),
-            vmem((layers, 2, ny, rows, fb // 2), BF16), vmem((layers, 2, ny, rows, fb // 2), BF16), vmem((layers, 2, ny, rows, fb // 2), BF16),
+            vmem((layers, 4, ny, rows, fb // 4), BF16), vmem((layers, 4, ny, rows, fb // 4), BF16), vmem((layers, 4, ny, rows, fb // 4), BF16),
             dma((7 + 8 * layers,)),
             dma((2 * layers, ny)), dma((2 * layers, ny)), dma((layers, 3, ny)), dma((layers, 3, ny)),
             dma((layers, ny)), dma((layers, ny)), dma((2 * layers,)), dma((2 * layers,)), dma((2 * layers, nx // 2)), dma((2 * layers, nx // 2)),
-            dma((2 * layers,)), dma((2 * layers,)), dma((layers, 2, ny)), dma((layers, 2, ny)), dma((layers, 2, ny)), dma((layers, 2, ny)),
+            dma((2 * layers,)), dma((2 * layers,)), dma((layers, 4, ny)), dma((layers, 4, ny)), dma((layers, 4, ny)), dma((layers, 4, ny)),
         ]
         cache_dims = (layers, rb, kl, hd)
         vmem_spec = pl.BlockSpec(memory_space=vmem)

time: 81.6 us -> 80.7 us (0.989)
  Pallas kernels: 80.9 us -> 79.8 us
    pallas_call x1, Pallas kernels: 77.5 us -> 76.4 us  [local_step(): pl.pallas_call(functools.partial(step_kernel, dims), out_shape=(vmem((row...]
where the time goes in v5:
time: 80.7 us; the launch traced here: 80.6 us
  Pallas kernels  79.8 us (99%)
  between operations  0.81 us (1%)
    pallas_call x1, Pallas kernels, local_step(): pl.pallas_call(functools.partial(step_kernel, dims), out_shape=(vmem((row...  76.4 us
    pallas_call x1, Pallas kernels, local_step(): pl.pallas_call(write_kernel, out_shape=(jax.ShapeDtypeStruct((rows, d_loc...  3.42 us

profile of v5, /device:TPU:97, one launch (start us, length us, event | category | flops | bytes accessed | tf_op | source)
XLA Modules:
  0.0 80.6 jit_solution(2825735637841119051)
XLA Ops:
  0.6 76.4 %decode_step.1 = (bf16[64,1024]{1,0:T(8,128)(2,1)S(1)}, bf16[2,16,512,128]{3,2,1,0:T(8,128)(2,1)S(1)}, bf16[2,16,512,128]{3,2,1,0:T(8,128)(2,1)S(1)}) custom-call(bf16[64,1024]{1,0:T(8,128)(2,1)} %hidden_in.1, s32[1,64]{1,0:T(1,128)} %bitcast.17, bf16[2,16,512,128]{3,2,1,0:T(8,128)(2,1)} %bitcast.10, bf16[2,16,512,128]{3,2,1,0:T(8,128)(2,1)} %bitcast.11, ...), custom_call_target="tpu_custom_call" | custom-call | tf_op jit(solution)/shard_map/decode_step/pallas_call | solution.py:476
  77.0 3.4 %cache_write.1 = (bf16[64,1024]{1,0:T(8,128)(2,1)}, bf16[2,16,512,128]{3,2,1,0:T(8,128)(2,1)}, bf16[2,16,512,128]{3,2,1,0:T(8,128)(2,1)}) custom-call(bf16[64,1024]{1,0:T(8,128)(2,1)S(1)} %get-tuple-element.9.hid_in, bf16[2,16,512,128]{3,2,1,0:T(8,128)(2,1)S(1)} %get-tuple-element.10.kc_in, bf16[2,16,512,128]{3,2,1,0:T(8,128)(2,1)S(1)} %get-tuple-element.11.vc_in), custom_call_target="tpu_custom_call" | custom-call | tf_op jit(solution)/shard_map/cache_write/pallas_call | solution.py:490

commit v6 on v5

--- a/solution.py
+++ b/solution.py
@@ -368,6 +368,7 @@
         for w in range(2):
             for d in y_order:
                 up_blocks(w, lax.rem(my + d, ny), up_tx)
+        for w in range(2):
             for hf in (2 * w, 2 * w + 1):
                 for d in y_order:
                     dst = lax.rem(my + d, ny)

time: 80.7 us -> 80.6 us (level)
  no operation moved by 1% of the time
where the time goes in v6:
time: 80.6 us; the launch traced here: 80.5 us
  Pallas kernels  79.9 us (99%)
    pallas_call x1, Pallas kernels, local_step(): pl.pallas_call(functools.partial(step_kernel, dims), out_shape=(vmem((row...  76.5 us
    pallas_call x1, Pallas kernels, local_step(): pl.pallas_call(write_kernel, out_shape=(jax.ShapeDtypeStruct((rows, d_loc...  3.42 us

profile of v6, /device:TPU:97, one launch (start us, length us, event | category | flops | bytes accessed | tf_op | source)
XLA Modules:
  0.0 80.5 jit_solution(1049993299897041709)
XLA Ops:
  0.6 76.5 %decode_step.1 = (bf16[64,1024]{1,0:T(8,128)(2,1)S(1)}, bf16[2,16,512,128]{3,2,1,0:T(8,128)(2,1)S(1)}, bf16[2,16,512,128]{3,2,1,0:T(8,128)(2,1)S(1)}) custom-call(bf16[64,1024]{1,0:T(8,128)(2,1)} %hidden_in.1, s32[1,64]{1,0:T(1,128)} %bitcast.17, bf16[2,16,512,128]{3,2,1,0:T(8,128)(2,1)} %bitcast.10, bf16[2,16,512,128]{3,2,1,0:T(8,128)(2,1)} %bitcast.11, ...), custom_call_target="tpu_custom_call" | custom-call | tf_op jit(solution)/shard_map/decode_step/pallas_call | solution.py:477
  77.1 3.4 %cache_write.1 = (bf16[64,1024]{1,0:T(8,128)(2,1)}, bf16[2,16,512,128]{3,2,1,0:T(8,128)(2,1)}, bf16[2,16,512,128]{3,2,1,0:T(8,128)(2,1)}) custom-call(bf16[64,1024]{1,0:T(8,128)(2,1)S(1)} %get-tuple-element.9.hid_in, bf16[2,16,512,128]{3,2,1,0:T(8,128)(2,1)S(1)} %get-tuple-element.10.kc_in, bf16[2,16,512,128]{3,2,1,0:T(8,128)(2,1)S(1)} %get-tuple-element.11.vc_in), custom_call_target="tpu_custom_call" | custom-call | tf_op jit(solution)/shard_map/cache_write/pallas_call | solution.py:491
